TPU v7x, 32 devices: a whole 2x2x4 slice. The times are simulated.
32 devices in a mesh: ma: 8 (over y, x, core), lev: 4 (over z).
Axes of the slice: x: 2, y: 2, z: 4, core: 2. Of those that a mesh axis runs over, the one named last changes fastest.
Arguments:
- spectral_state: float32 [1280, 2, 16, 1280], P('ma', None, None, 'lev'), may hold values from -6 to 6
- forcing_noise: bfloat16 [1280, 2, 16, 1280], P('ma', None, None, 'lev'), may hold values from -6 to 6
- decay_rate: float32 [16], replicated, may hold values from 0.3 to 0.95
- amplitude: float32 [1280], P('lev'), may hold values from 0.2 to 2
- legendre: bfloat16 [1280, 1280, 640], P('ma', 'lev'), may hold values from -0.0048828125 to 0.0048828125
- wave_of_slot: int32 [1280], replicated, may hold values from 0 to 1279, each once
- lat_of_row: int32 [1280], replicated, may hold values from 0 to 1279, each once
Outputs:
- new_state: float32 [1280, 2, 16, 1280], P('ma', None, None, 'lev')
- pattern: bfloat16 [16, 1280, 2560], P('lev', 'ma')
Inputs may be any that keep to these rules, and one draw needn't show every extreme that they name: `wave_of_slot`: each zonal wavenumber is held by exactly one slot. `lat_of_row`: each latitude is held by exactly one row.
All inputs are finite; a program needn't handle non-finite values.
Results may differ from a plain program's by a relative error of at most 0.014.
Values may be sent and summed in bfloat16 or wider, within the bound.
No kernel may reach another device: no remote copies, remote signals or barrier semaphores. Data moves between devices by JAX's collectives and lax.ppermute only.
A program may use at most 192 MiB of HBM per device.

v0:
```python
import math

import jax
import jax.numpy as jnp
from jax import lax
from jax.sharding import PartitionSpec as P

NLON = 2560


def build_table(wavenum, width):
    column = jnp.arange(width, dtype=jnp.int32)
    product = wavenum[:, None] * column[None, :] % width
    phase_angle = product.astype(jnp.float32) * jnp.float32(2.0 * math.pi / width)
    factor = jnp.where(wavenum == 0, jnp.float32(1.0), jnp.float32(2.0))[:, None]
    stacked = jnp.stack([factor * jnp.cos(phase_angle), -factor * jnp.sin(phase_angle)], axis=1)
    return stacked.astype(jnp.bfloat16)


def body(spectral_state, forcing_noise, decay_rate, amplitude, legendre, wave_of_slot, lat_of_row):
    slot_count = spectral_state.shape[0]
    level_count = spectral_state.shape[2]
    width_n = spectral_state.shape[3]
    lat_count = lat_of_row.shape[0]
    first_slot = lax.axis_index("ma") * slot_count
    wavenum = lax.dynamic_slice_in_dim(wave_of_slot, first_slot, slot_count)
    total_n = lax.axis_index("lev") * width_n + jnp.arange(width_n, dtype=jnp.int32)
    valid_mask = total_n[None, :] >= wavenum[:, None]
    updated = decay_rate[None, None, :, None] * spectral_state + amplitude[
        None, None, None, :
    ] * forcing_noise.astype(jnp.float32)
    new_state = jnp.where(valid_mask[:, None, None, :], updated, jnp.float32(0.0))
    spectral = new_state.astype(jnp.bfloat16).reshape(slot_count, 2 * level_count, width_n)
    odd_mask = ((total_n[None, :] - wavenum[:, None]) % 2 == 1)[:, None, :]
    even_part = jnp.where(odd_mask, jnp.zeros_like(spectral), spectral)
    odd_part = jnp.where(odd_mask, spectral, jnp.zeros_like(spectral))
    stacked = jnp.concatenate([even_part, odd_part], axis=1)
    halves = jnp.einsum("scn,snj->scj", stacked, legendre, preferred_element_type=jnp.float32)
    even_sum = halves[:, : 2 * level_count]
    odd_sum = halves[:, 2 * level_count :]
    north = (even_sum + odd_sum).astype(jnp.bfloat16)
    south = (even_sum - odd_sum).astype(jnp.bfloat16)
    full = jnp.concatenate([north, jnp.flip(south, axis=2)], axis=2).reshape(
        slot_count, 2, level_count, lat_count
    )
    summed = (
        lax.psum_scatter(full, "lev", scatter_dimension=2, tiled=True)
        .astype(jnp.float32)
        .astype(jnp.bfloat16)
    )
    by_row = jnp.take(summed, lat_of_row, axis=3)
    fourier = lax.all_to_all(by_row, "ma", split_axis=3, concat_axis=0, tiled=True)
    dft_table = build_table(wave_of_slot, NLON)
    pattern = jnp.einsum("srlk,srx->lkx", fourier, dft_table, preferred_element_type=jnp.float32)
    return (new_state, pattern.astype(jnp.bfloat16))


def solution(mesh):
    return jax.shard_map(
        body,
        mesh=mesh,
        in_specs=(
            P("ma", None, None, "lev"),
            P("ma", None, None, "lev"),
            P(),
            P("lev"),
            P("ma", "lev", None),
            P(),
            P(),
        ),
        out_specs=(P("ma", None, None, "lev"), P("lev", "ma", None)),
        check_vma=False,
    )
```

profile of v0, /device:TPU:0, one launch (start us, length us, event | category | flops | bytes accessed | tf_op | source)
XLA Modules:
  0.0 453.0 jit_solution(9363080196011248048)
XLA Ops:
  7.2 0.0 reduce-scatter.2.cloned.1.call-start
  7.2 0.8 dynamic_slice.3
  8.0 0.2 broadcast_compare_fusion
  8.2 7.5 %bitcast_select_fusion.1 = (bf16[160,32,320]{2,1,0:T(8,128)(2,1)}, f32[160,2,16,320]{3,2,1,0:T(8,128)S(1)}) fusion(pred[160,320]{1,0:T(8,128)(4,1)S(1)} %get-tuple-element.11, bf16[160,2,16,320]{3,2,1,0:T(8,128)(2,1)} %param.8, f32[320]{0:T(512)} %param.10, f32[160,2,16,320]{3,2,1,0:T(8,128)} %param.7, f32[16]{0:T(128)} %param.9, ...), kind=kLoop, calls=%fused_computation.26 | loop fusion | flops 11468800 | bytes 19764544 | tf_op jit(solution)/shard_map/jit(_where)/select_n | solution.py:35
  15.7 0.0 copy-start
  15.7 3.2 copy-done
  18.9 2.7 bitcast_select_fusion
  21.6 34.1 %fusion.8 = f32[160,64,640]{2,1,0:T(8,128)} fusion(bf16[160,320,640]{2,1,0:T(8,128)(2,1)} %param.11, bf16[160,32,320]{2,1,0:T(8,128)(2,1)} %bitcast_select_fusion, bf16[160,32,320]{2,1,0:T(8,128)(2,1)} %get-tuple-element.2), kind=kOutput, calls=%fused_computation.17 | convolution fusion | flops 4207411200 | bytes 98304000 | tf_op jit(solution)/shard_map/scn,snj->scj/dot_general | solution.py:38
  55.6 13.4 %add_convert_fusion = (bf16[160,32,640]{2,1,0:T(8,128)(2,1)}, bf16[160,32,640]{2,1,0:T(8,128)(2,1)}) fusion(f32[160,64,640]{2,1,0:T(8,128)} %fusion.8), kind=kLoop, calls=%fused_computation.15 | loop fusion | flops 13107200 | bytes 39321600 | tf_op jit(solution)/shard_map/convert_element_type | solution.py:41
  69.0 16.6 %rev.4 = bf16[160,32,640]{2,1,0:T(8,128)(2,1)} reverse(bf16[160,32,640]{2,1,0:T(8,128)(2,1)} %get-tuple-element.5), dimensions={2} | reverse | bytes 13107200 | tf_op jit(solution)/shard_map/jit(_flip)/rev | solution.py:43
  85.7 6.4 %pad_maximum_fusion = bf16[160,32,1280]{2,1,0:T(8,128)(2,1)S(1)} fusion(bf16[160,32,640]{2,1,0:T(8,128)(2,1)} %rev.4, bf16[160,32,640]{2,1,0:T(8,128)(2,1)} %get-tuple-element.4), kind=kLoop, calls=%fused_computation.4 | loop fusion | flops 26214400 | bytes 26214400 | tf_op jit(solution)/shard_map/concatenate | solution.py:43
  92.1 9.4 %copy.12 = bf16[160,2,16,1280]{3,0,1,2:T(8,128)(2,1)} copy(bf16[160,2,16,1280]{3,2,1,0:T(8,128)(2,1)S(1)} %bitcast.24) | data formatting | bytes 26214400 | tf_op jit(solution)/shard_map/reshape | solution.py:43
  101.4 0.0 copy-start.2
  101.4 0.0 reduce-scatter.2.cloned.1.call-update
  101.5 0.7 copy-done.2
  102.2 222.5 %reduce-scatter.2.cloned.1.call-done = bf16[160,2,4,1280]{3,0,1,2:T(8,128)(2,1)} async-done(((bf16[160,2,16,1280]{3,0,1,2:T(8,128)(2,1)}), bf16[160,2,4,1280]{3,0,1,2:T(8,128)(2,1)}) %reduce-scatter.2.cloned.1.call-update) | async-done | bytes 3276816 | tf_op jit(solution)/shard_map/reduce_scatter | solution.py:47
  324.7 8.5 %copy.13 = bf16[160,2,4,1280]{0,2,3,1:T(4,128)(2,1)} copy(bf16[160,2,4,1280]{3,0,1,2:T(8,128)(2,1)} %reduce-scatter.2.cloned.1.call-done) | data formatting | bytes 6553600 | tf_op jit(solution)/shard_map/reduce_scatter | solution.py:47
  333.2 10.8 %gather_fusion = bf16[1280,160,2,4]{1,3,2,0:T(4,128)(2,1)} fusion(bf16[160,2,4,1280]{0,2,3,1:T(4,128)(2,1)} %copy.13, s32[2048]{0:T(1024)S(1)} %pad_clamp_fusion), kind=kCustom, calls=%fused_computation | custom fusion | bytes 6558720 | tf_op jit(solution)/shard_map/jit(_take)/gather | solution.py:51
  344.0 8.2 %select_bitcast_fusion = bf16[160,2,4,1280]{0,2,1,3:T(4,128)(2,1)} fusion(bf16[1280,160,2,4]{1,3,2,0:T(4,128)(2,1)} %gather_fusion, pred[1280]{0:T(1024)(128)(4,1)S(1)} %compare_and_fusion), kind=kLoop, calls=%fused_computation.24 | loop fusion | flops 1638400 | bytes 6554880 | tf_op jit(solution)/shard_map/jit(_take)/select_n | solution.py:51
  352.2 0.0 copy-start.1
  352.2 5.0 %all-to-all-start = ((bf16[160,2,4,1280]{0,2,1,3:T(4,128)(2,1)}), bf16[160,2,4,1280]{0,2,1,3:T(4,128)(2,1)}, u32[]{:S(2)}, u32[]{:S(2)}) async-start(bf16[160,2,4,1280]{0,2,1,3:T(4,128)(2,1)} %select_bitcast_fusion), calls=%async_computation.1 | async-start | bytes 10485760 | tf_op jit(solution)/shard_map/all_to_all | solution.py:52
  357.1 0.0 copy-done.1
  357.2 58.1 %multiply_convert_fusion.1 = (bf16[1280,1,2560]{2,0,1:T(8,128)(2,1)}, bf16[1280,1,2560]{2,0,1:T(8,128)(2,1)}) fusion(s32[1280]{0:T(1024)S(1)} %copy-done.1, f32[1280]{0:T(1024)S(1)} %get-tuple-element.8, f32[1280]{0:T(1024)S(1)} %get-tuple-element.9), kind=kLoop, calls=%fused_computation.10 | loop fusion | flops 42598400 | bytes 13122560 | tf_op jit(solution)/shard_map/convert
  415.3 2.2 all-to-all-done
  417.5 7.8 %copy.17 = bf16[160,2,4,8,160]{0,3,4,1,2:T(8,128)(2,1)} copy(bf16[160,2,4,8,160]{0,2,1,4,3:T(4,128)(2,1)} %bitcast.3) | data formatting | bytes 6553600 | tf_op jit(solution)/shard_map/all_to_all | solution.py:52
  425.3 8.0 %all_to_all.16 = bf16[1280,2,4,160]{0,3,1,2:T(8,128)(2,1)S(1)} reshape(bf16[8,160,2,4,160]{1,0,4,2,3:T(8,128)(2,1)} %bitcast.25) | data formatting | bytes 6553600 | tf_op jit(solution)/shard_map/all_to_all | solution.py:52
  433.2 12.9 %bitcast_convert_fusion = bf16[4,160,2560]{2,1,0:T(8,128)(2,1)} fusion(bf16[1280,2,4,160]{0,3,1,2:T(8,128)(2,1)S(1)} %all_to_all.16, bf16[1280,1,2560]{2,0,1:T(8,128)(2,1)} %get-tuple-element.7, bf16[1280,1,2560]{2,0,1:T(8,128)(2,1)} %get-tuple-element.6), kind=kOutput, calls=%fused_computation.22 | convolution fusion | flops 8396800000 | bytes 19660800 | tf_op jit(solution)/shard_map/srlk,srx->lkx/dot_general | solution.py:54
  (5 shorter events, 0.0 us)
Async XLA Ops:
  7.2 317.5 %reduce-scatter.2.cloned.1.call-start = ((), (), s32[]{:S(2)}) async-start(), calls=%async_computation.2 | async-start | bytes 16384000 | tf_op jit(solution)/shard_map/reduce_scatter | solution.py:47
  15.7 3.2 copy-start
  101.4 0.7 copy-start.2
  352.2 5.0 %copy-start.1 = (s32[1280]{0:T(1024)S(1)}, s32[1280]{0:T(1024)}, u32[]{:S(2)}) copy-start(s32[1280]{0:T(1024)} %param.12) | copy-start | bytes 15364
  352.2 65.3 %all-to-all-start = ((bf16[160,2,4,1280]{0,2,1,3:T(4,128)(2,1)}), bf16[160,2,4,1280]{0,2,1,3:T(4,128)(2,1)}, u32[]{:S(2)}, u32[]{:S(2)}) async-start(bf16[160,2,4,1280]{0,2,1,3:T(4,128)(2,1)} %select_bitcast_fusion), calls=%async_computation.1 | async-start | bytes 10485760 | tf_op jit(solution)/shard_map/all_to_all | solution.py:52
Sparse Core Ops, SparseCore 0:
  101.6 223.0 reduce-scatter.1
where the time goes:
time: 454 us; the launch traced here: 453 us
  waiting for transfers between devices  225 us (50%)
  other arithmetic  96.5 us (21%)
  local copies, waits for them, and re-layouts  65.7 us (14%)
  matrix products  47 us (10%)
  between operations  14.1 us (3%)
  starting transfers between devices  5.01 us (1%)
    reduce_scatter x1, waiting for transfers between devices, body(): lax.psum_scatter(full, 'lev', scatter_dimension=2, tiled=True)  223 us
    another operation x1, other arithmetic  58.1 us
    dot_general x1, matrix products, body(): jnp.einsum('scn,snj->scj', stacked, legendre, preferred_element_type=jnp....  34.1 us
    rev x1, local copies, waits for them, and re-layouts, body(): jnp.flip(south, axis=2)  16.6 us
    all_to_all x2, local copies, waits for them, and re-layouts, body(): lax.all_to_all(by_row, 'ma', split_axis=3, concat_axis=0, tiled=True)  15.8 us
    convert_element_type x1, other arithmetic, body(): north = (even_sum + odd_sum).astype(jnp.bfloat16)  13.4 us
    dot_general x1, matrix products, body(): jnp.einsum('srlk,srx->lkx', fourier, dft_table, preferred_element_type=jn...  12.9 us
    gather x1, local copies, waits for them, and re-layouts, body(): by_row = jnp.take(summed, lat_of_row, axis=3)  10.8 us
  transfers between devices with their start and end apart: 2, of which 2 were waited for; matrix products, arithmetic and copies ran while one was open for 13% of the time, Pallas kernels for 0%

commit v1 on v0

v1 whole, which is shorter than its diff:
```python
import functools
import math

import jax
import jax.numpy as jnp
from jax import lax
from jax.experimental import pallas as pl
from jax.experimental.pallas import tpu as pltpu
from jax.sharding import PartitionSpec as P


MIB = 2**20
TAIL, HEAD = (0, 1), (2, 3)


def table_kernel(width, wave, out):
    count = wave.shape[1]
    number = wave[0]
    column = lax.broadcasted_iota(jnp.int32, (count, 128), 1)
    scale = jnp.float32(2.0 * math.pi / width)

    def angle(product):
        real = product.astype(jnp.float32)
        turns = (real * jnp.float32(1.0 / width)).astype(jnp.int32)
        return (product - turns * width).astype(jnp.float32) * scale

    fine = angle(number * column)
    coarse = angle(number * (column * 128))
    factor = jnp.where(number == 0, 1.0, 2.0).astype(jnp.float32)
    fine_cos, fine_sin = factor * jnp.cos(fine), factor * jnp.sin(fine)
    coarse_cos, coarse_sin = jnp.cos(coarse), jnp.sin(coarse)
    for t in range(width // 128):
        c, s = coarse_cos[:, t : t + 1], coarse_sin[:, t : t + 1]
        lanes = pl.ds(t * 128, 128)
        out[0, pl.ds(0, count), lanes] = (c * fine_cos - s * fine_sin).astype(out.dtype)
        out[0, pl.ds(count, count), lanes] = -(s * fine_cos + c * fine_sin).astype(out.dtype)


def table_group(wavenum, width):
    owners, count = wavenum.shape
    wide = jnp.broadcast_to(wavenum[:, :, None], (owners, count, 128))
    return pl.pallas_call(
        functools.partial(table_kernel, width),
        grid=(owners,),
        in_specs=[pl.BlockSpec((1, count, 128), lambda s: (s, 0, 0))],
        out_specs=pl.BlockSpec((1, 2 * count, width), lambda s: (s, 0, 0)),
        out_shape=jax.ShapeDtypeStruct((owners, 2 * count, width), jnp.bfloat16),
        cost_estimate=pl.CostEstimate(
            flops=16 * owners * count * width,
            bytes_accessed=4 * owners * count * width,
            transcendentals=0,
        ),
        name="table",
    )(wide)


def legendre_kernel(first, slots, n_lev, lv, chained, wave, rate, amp, state, noise, leg, *rest):
    if chained:
        rest = rest[1:]
    new_state, pieces, (far, decay, turn) = rest[0], rest[1:-3], rest[-3:]
    step = pl.program_id(0)
    block, width = state.shape[0], state.shape[3]
    half = leg.shape[2]
    dev = lax.axis_index("lev")
    lead_slot = lax.axis_index("ma") * slots + first + step * block
    rows = 2 * lv

    @pl.when(step == 0)
    def _():
        for l in range(n_lev * lv):
            decay[pl.ds(l, 1), :] = jnp.full((1, width), rate[l], jnp.float32)

    total_n = lax.broadcasted_iota(jnp.int32, (1, width), 1) + dev * width
    gain = amp[...].reshape(1, width)
    signs = []
    for i in range(block):
        offset = total_n - wave[lead_slot + i]
        valid = offset >= 0
        signs.append(jnp.where((offset & 1) == 1, -1.0, 1.0).astype(jnp.float32))
        parts = []
        for p in range(2):
            value = decay[...] * state[i, p] + gain * noise[i, p].astype(jnp.float32)
            value = jnp.where(valid, value, 0.0)
            new_state[i, p] = value
            parts.append(value)
        order = jnp.concatenate(
            [parts[p][j * lv : (j + 1) * lv] for j in range(n_lev) for p in range(2)], axis=0
        )
        turn[i, pl.ds(0, n_lev * rows), :] = order
        turn[i, pl.ds(n_lev * rows, n_lev * rows), :] = order
    lead = pl.multiple_of(dev * rows, rows)
    held = []
    for i in range(block):
        coeff = turn[i, pl.ds(lead, n_lev * rows), :]
        lhs = jnp.concatenate([coeff, coeff * signs[i]], axis=0).astype(jnp.bfloat16)
        held.append(jnp.dot(lhs, leg[i], preferred_element_type=jnp.float32))
        if i % 2 == 1:
            for k in range(n_lev):
                at = pl.ds((i - 1) * rows, 2 * rows)
                for side in range(2):
                    base = side * n_lev * rows + k * rows
                    pair = jnp.concatenate([h[base : base + rows] for h in held], axis=0)
                    pair = pair.astype(jnp.bfloat16)
                    pieces[k][at, pl.ds(side * half, half)] = pair
                    if k in (1, n_lev - 1):

                        @pl.when((k == 1) == (dev == n_lev - 1))
                        def _():
                            far[at, pl.ds(side * half, half)] = pair

            held = []


def legendre_group(first, count, n_lev, wave, rate, amp, state, noise, leg, chain):
    slots, _, level_count, width = state.shape
    half = leg.shape[2]
    lv = level_count // n_lev
    rows = 2 * lv
    sb = next(b for b in (16, 8, 4, 2) if first % b == 0 and count % (2 * b) in (0, b) and count > b)
    base = first // sb
    chained = chain is not None
    four = lambda s, *_: (base + s, 0, 0, 0)
    in_specs = [
        pl.BlockSpec((width,), lambda s, *_: (0,)),
        pl.BlockSpec((sb, 2, level_count, width), four),
        pl.BlockSpec((sb, 2, level_count, width), four),
        pl.BlockSpec((sb, width, half), lambda s, *_: (base + s, 0, 0)),
    ]
    args = [wave, rate, amp, state, noise, leg]
    if chained:
        in_specs.append(pl.BlockSpec(memory_space=pl.ANY))
        args.append(chain)
    out = pl.pallas_call(
        functools.partial(legendre_kernel, first, slots, n_lev, lv, chained),
        grid_spec=pltpu.PrefetchScalarGridSpec(
            num_scalar_prefetch=2,
            grid=(count // sb,),
            in_specs=in_specs,
            out_specs=[pl.BlockSpec((sb, 2, level_count, width), four)]
            + [pl.BlockSpec((sb * rows, 2 * half), lambda s, *_: (s, 0))] * (n_lev + 1),
            scratch_shapes=[
                pltpu.VMEM((level_count, width), jnp.float32),
                pltpu.VMEM((sb, 2 * n_lev * rows, width), jnp.float32),
            ],
        ),
        out_shape=[jax.ShapeDtypeStruct(state.shape, jnp.float32)]
        + [jax.ShapeDtypeStruct((count * rows, 2 * half), jnp.bfloat16)] * (n_lev + 1),
        input_output_aliases={6: 0} if chained else {},
        cost_estimate=pl.CostEstimate(
            flops=4 * count * n_lev * rows * width * half,
            bytes_accessed=count * width * (half * 2 + 10 * n_lev * rows),
            transcendentals=0,
        ),
    )(*args)
    return out[0], out[1:]


def rows_kernel(lv, *refs):
    addends, (pick, out, total, ready) = refs[:-4], refs[-4:]
    own = addends[0]
    rows = 2 * lv
    count = own.shape[0] // rows
    owners, per, chunk = out.shape

    @pl.when(pl.program_id(0) == 0)
    def _():
        for t in range(own.shape[1] // 128):
            lanes = pl.ds(t * 128, 128)
            value = own[:, lanes].astype(jnp.float32)
            for other in addends[1:]:
                value = value + other[:, lanes].astype(jnp.float32)
            total[t] = value
            for l in range(lv):
                for p in range(2):
                    some = total[t, pl.ds(p * lv + l, count, stride=rows), :]
                    ready[pl.ds((2 * l + p) * count, count), lanes] = some.astype(jnp.bfloat16)

    mine = ready[pl.ds(pl.multiple_of(pl.program_id(0) * chunk, chunk), chunk), :]
    out[...] = (
        lax.dot_general(
            pick[...], mine, (((1,), (1,)), ((), ())), preferred_element_type=jnp.float32
        )
        .astype(jnp.bfloat16)
        .reshape(owners, per, chunk)
    )


def rows_group(n_ma, lv, addends, pick):
    own = addends[0]
    lat_count = pick.shape[0]
    per = lat_count // n_ma
    n_rows = own.shape[0]
    chunk = 256 if n_rows % 256 == 0 else n_rows
    whole = pl.BlockSpec(own.shape, lambda s: (0, 0))
    return pl.pallas_call(
        functools.partial(rows_kernel, lv),
        grid=(n_rows // chunk,),
        in_specs=[whole] * len(addends) + [pl.BlockSpec(pick.shape, lambda s: (0, 0))],
        out_specs=pl.BlockSpec((n_ma, per, chunk), lambda s: (0, 0, s)),
        out_shape=jax.ShapeDtypeStruct((n_ma, per, n_rows), jnp.bfloat16),
        scratch_shapes=[
            pltpu.VMEM((own.shape[1] // 128, n_rows, 128), jnp.float32),
            pltpu.VMEM(own.shape, jnp.bfloat16),
        ],
        cost_estimate=pl.CostEstimate(
            flops=2 * n_rows * lat_count * lat_count,
            bytes_accessed=8 * n_rows * lat_count + 2 * lat_count * lat_count,
            transcendentals=0,
        ),
        compiler_params=pltpu.CompilerParams(vmem_limit_bytes=24 * MIB),
        name="rows",
    )(*addends, pick)


def wave_kernel(lv, counts, has_acc, *refs):
    total = sum(counts)
    tables = refs[total : total + len(counts)]
    end = total + len(counts) + has_acc
    out, lhs = refs[end], refs[end + 1 :]
    owners, per, _ = refs[0].shape

    @pl.when(pl.program_id(0) == 0)
    def _():
        at = 0
        for count, left in zip(counts, lhs):
            spectra = refs[at : at + count]
            at += count
            depth = spectra[0].shape[2] // lv
            for o in range(owners):
                value = spectra[0][o]
                if count > 1:
                    value = sum(x[o].astype(jnp.float32) for x in spectra).astype(value.dtype)
                for l in range(lv):
                    left[pl.ds(l * per, per), pl.ds(o * depth, depth)] = value[
                        :, l * depth : (l + 1) * depth
                    ]

    value = None
    for table, left in zip(tables, lhs):
        part = jnp.dot(
            left[...],
            table[...].reshape(left.shape[1], table.shape[2]),
            preferred_element_type=jnp.float32,
        )
        value = part if value is None else value + part
    value = value.reshape(out.shape)
    if has_acc:
        value = value + refs[end - 1][...]
    out[...] = value.astype(out.dtype)


def wave_group(lv, spectra, tables, acc, dtype):
    owners, per, _ = spectra[0][0].shape
    width = tables[0].shape[-1]
    xb = width // 5
    in_specs = [pl.BlockSpec(x.shape, lambda s: (0, 0, 0)) for xs in spectra for x in xs]
    in_specs += [pl.BlockSpec((owners, t.shape[1], xb), lambda s: (0, 0, s)) for t in tables]
    sheet = pl.BlockSpec((lv, per, xb), lambda s: (0, 0, s))
    added = [] if acc is None else [acc]
    depth = sum(owners * t.shape[1] for t in tables)
    return pl.pallas_call(
        functools.partial(wave_kernel, lv, tuple(len(xs) for xs in spectra), len(added)),
        grid=(width // xb,),
        in_specs=in_specs + [sheet] * len(added),
        out_specs=sheet,
        out_shape=jax.ShapeDtypeStruct((lv, per, width), dtype),
        scratch_shapes=[
            pltpu.VMEM((lv * per, owners * t.shape[1]), jnp.bfloat16) for t in tables
        ],
        cost_estimate=pl.CostEstimate(
            flops=2 * lv * per * depth * width,
            bytes_accessed=width * (2 * lv * per + 2 * depth),
            transcendentals=0,
        ),
        compiler_params=pltpu.CompilerParams(vmem_limit_bytes=60 * MIB),
        name="wave",
    )(*[x for xs in spectra for x in xs], *tables, *added)


def plan(slots):
    return [part * slots // 10 for part in (1, 2, 4, 3)]


def body(n_ma, n_lev, state, noise, decay_rate, amplitude, legendre, wave_of_slot, lat_of_row):
    slots, _, level_count, _ = state.shape
    half = legendre.shape[2]
    lat_count = lat_of_row.shape[0]
    lv = level_count // n_lev
    sizes = plan(slots)
    firsts = [sum(sizes[:g]) for g in range(len(sizes))]
    groups = list(range(len(sizes)))

    chain = None
    pieces = []
    for g in groups:
        chain, out = legendre_group(
            firsts[g], sizes[g], n_lev, wave_of_slot, decay_rate, amplitude,
            state, noise, legendre, chain,
        )
        pieces.append(out)

    column = jnp.where(lat_of_row < half, lat_of_row, 3 * half - 1 - lat_of_row)
    number = jnp.arange(lat_count, dtype=jnp.int32)
    pick = (column[:, None] == number[None, :]).astype(jnp.bfloat16)

    def exchange(addends):
        spectrum = rows_group(n_ma, lv, addends, pick)
        return lax.all_to_all(spectrum, "ma", split_axis=0, concat_axis=0, tiled=True)

    def send(value, pairs):
        return lax.ppermute(value, "lev", pairs)

    from_above = [None] * len(sizes)
    from_below = [None] * len(sizes)
    for phase in range(n_lev - 1):
        last = phase == n_lev - 2
        dist = n_lev - 1 - phase
        down = [(i, i - 1) for i in range(dist, n_lev)]
        up = [(i, i + 1) for i in range(n_lev - dist)]
        lows, highs = {}, {}
        for g in groups:
            if phase == 0:
                from_above[g] = send(pieces[g][n_lev], down + up)
                from_below[g] = from_above[g]
                continue
            lows[g] = pieces[g][n_lev - dist] + from_above[g]
            highs[g] = pieces[g][dist] + from_below[g]
            if not last:
                from_above[g] = send(lows[g], down)
                from_below[g] = send(highs[g], up)
    for g in HEAD:
        from_above[g] = send(lows[g], down)
        from_below[g] = send(highs[g], up)
    join = lambda xs: jnp.concatenate([xs[g] for g in TAIL], axis=0)
    tail_own = exchange([join({g: pieces[g][0] for g in TAIL})])
    tail_low = exchange([join(lows)])
    tail_high = exchange([join(highs)])
    tail_low = send(tail_low, down)
    tail_high = send(tail_high, up)

    by_owner = wave_of_slot.reshape(n_ma, slots)
    spectra, tables = [], []
    for g in HEAD:
        spectra.append([exchange([pieces[g][0], from_above[g], from_below[g]])])
        tables.append(
            table_group(by_owner[:, firsts[g] : firsts[g] + sizes[g]], 2 * lat_count)
        )
    spectra.append([tail_own, tail_low, tail_high])
    tables.append(table_group(by_owner[:, : firsts[HEAD[0]]], 2 * lat_count))
    late = len(HEAD) - 1
    rest = [q for q in range(len(spectra)) if q != late]
    acc = wave_group(lv, [spectra[q] for q in rest], [tables[q] for q in rest], None, jnp.float32)
    pattern = wave_group(lv, [spectra[late]], [tables[late]], acc, jnp.bfloat16)
    return chain, pattern


def solution(mesh):
    n_lev = mesh.shape["lev"]

    def inner(*args):
        return body(mesh.shape["ma"], n_lev, *args)

    return jax.shard_map(
        inner,
        mesh=mesh,
        in_specs=(
            P("ma", None, None, "lev"),
            P("ma", None, None, "lev"),
            P(),
            P("lev"),
            P("ma", "lev", None),
            P(),
            P(),
        ),
        out_specs=(P("ma", None, None, "lev"), P("lev", "ma", None)),
        check_vma=False,
    )
```

time: 454 us -> 305 us (0.67)
  waiting for transfers between devices: 225 us -> 84.3 us
  Pallas kernels: 0 us -> 109 us
  other arithmetic: 96.5 us -> 20.8 us
  starting transfers between devices: 5.01 us -> 77.5 us
  local copies, waits for them, and re-layouts: 65.7 us -> 9.77 us
  matrix products: 47 us -> 0 us
  between operations: 14.1 us -> 0.99 us
    reduce_scatter x1 -> x0, waiting for transfers between devices: 223 us -> none  [body(): lax.psum_scatter(full, 'lev', scatter_dimension=2, tiled=True)]
    pallas_call x0 -> x14, Pallas kernels: none -> 109 us  [the longest x4 51.9 us: legendre_group(): pl.pallas_call(functools.partial(legendre_kernel, first, slots, n_lev, lv...]
    ppermute x0 -> x18, waiting for transfers between devices: none -> 84.3 us  [send(): return lax.ppermute(value, 'lev', pairs)]
    another operation x1 -> x0, other arithmetic: 58.1 us -> none
    ppermute x0 -> x18, starting transfers between devices: none -> 56.6 us  [send(): return lax.ppermute(value, 'lev', pairs)]
    dot_general x2 -> x0, matrix products: 47 us -> none  [the longest x1 34.1 us: body(): jnp.einsum('scn,snj->scj', stacked, legendre, preferred_element_type=jnp....]
    add x1 -> x12, other arithmetic: 0.01 us -> 20 us  [the longest x8 12.5 us: body(): lows[g] = pieces[g][n_lev - dist] + from_above[g]]
    select_n x5 -> x1, other arithmetic: 18.3 us -> 0.01 us  [body(): column = jnp.where(lat_of_row < half, lat_of_row, 3 * half - 1 - lat_of_row)]
  transfers between devices with their start and end apart: 2 -> 23, of which waited for: 2 -> 7; matrix products, arithmetic and copies ran while one was open for 13% -> 8% of each run, Pallas kernels for 0% -> 21%
where the time goes in v1:
time: 305 us; the launch traced here: 302 us
  Pallas kernels  109 us (36%)
  waiting for transfers between devices  84.3 us (28%)
  starting transfers between devices  77.5 us (25%)
  other arithmetic  20.8 us (7%)
  local copies, waits for them, and re-layouts  9.77 us (3%)
    ppermute x18, waiting for transfers between devices, send(): return lax.ppermute(value, 'lev', pairs)  84.3 us
    ppermute x18, starting transfers between devices, send(): return lax.ppermute(value, 'lev', pairs)  56.6 us
    pallas_call x4, Pallas kernels, legendre_group(): pl.pallas_call(functools.partial(legendre_kernel, first, slots, n_lev, lv...  51.9 us
    pallas_call x2, Pallas kernels, wave_group(): pl.pallas_call(functools.partial(wave_kernel, lv, tuple((len(xs) for xs i...  22.4 us
    pallas_call x3, Pallas kernels, table_group(): pl.pallas_call(functools.partial(table_kernel, width), grid=(owners,), in...  21.1 us
    all_to_all x5, starting transfers between devices, exchange(): lax.all_to_all(spectrum, 'ma', split_axis=0, concat_axis=0, tiled=True)  20.9 us
    pallas_call x5, Pallas kernels, rows_group(): pl.pallas_call(functools.partial(rows_kernel, lv), grid=(n_rows // chunk,...  13.6 us
    add x8, other arithmetic, body(): lows[g] = pieces[g][n_lev - dist] + from_above[g]  12.5 us
  transfers between devices with their start and end apart: 23, of which 7 were waited for; matrix products, arithmetic and copies ran while one was open for 8% of the time, Pallas kernels for 21%

profile of v1, /device:TPU:0, one launch (start us, length us, event | category | flops | bytes accessed | tf_op | source)
XLA Modules:
  0.0 302.5 jit_solution(9244475512059259574)
XLA Ops:
  0.6 6.7 %shard_map.86 = (f32[160,2,16,320]{3,2,1,0:T(8,128)}, bf16[128,1280]{1,0:T(8,128)(2,1)}, bf16[128,1280]{1,0:T(8,128)(2,1)}, bf16[128,1280]{1,0:T(8,128)(2,1)}, b...) custom-call(s32[1280]{0:T(1024)} %wave.9, f32[16]{0:T(128)} %rate.7, f32[320]{0:T(512)} %amp.7, ...), custom_call_target="tpu_custom_call" | custom-call | flops 419430400 | bytes 8192000 | tf_op jit(solution)/shard_map/pallas_call | solution.py:133
  7.3 10.9 %shard_map.87 = (f32[160,2,16,320]{3,2,1,0:T(8,128)}, bf16[256,1280]{1,0:T(8,128)(2,1)}, bf16[256,1280]{1,0:T(8,128)(2,1)}, bf16[256,1280]{1,0:T(8,128)(2,1)}, b...) custom-call(s32[1280]{0:T(1024)} %wave.9, f32[16]{0:T(128)} %rate.7, ...), custom_call_target="tpu_custom_call", output_to_operand_aliasing={{0}: (6, {})} | custom-call | flops 838860800 | bytes 16384000 | tf_op jit(solution)/shard_map/pallas_call | solution.py:133
  18.2 18.6 %shard_map.88 = (f32[160,2,16,320]{3,2,1,0:T(8,128)}, bf16[512,1280]{1,0:T(8,128)(2,1)}, bf16[512,1280]{1,0:T(8,128)(2,1)}, bf16[512,1280]{1,0:T(8,128)(2,1)}, b...) custom-call(s32[1280]{0:T(1024)} %wave.9, f32[16]{0:T(128)} %rate.7, ...), custom_call_target="tpu_custom_call", output_to_operand_aliasing={{0}: (6, {})} | custom-call | flops 1677721600 | bytes 32768000 | tf_op jit(solution)/shard_map/pallas_call | solution.py:133
  36.8 5.1 %collective-permute-start.5 = (bf16[512,1280]{1,0:T(8,128)(2,1)}, bf16[512,1280]{1,0:T(8,128)(2,1)S(1)}, u32[]{:S(2)}, u32[]{:S(2)}) collective-permute-start(bf16[512,1280]{1,0:T(8,128)(2,1)} %get-tuple-element.38), channel_id=1, source_target_pairs={{3,2},{0,1},{7,6},{4,5},{11,10},{8,9},{15,14},{12,13},{19,18},{16,... | collective-permute-start | bytes 3932168 | tf_op jit(solution)/shard_map/ppermute | solution.py:311
  45.9 39.4 %collective-permute-done.12 = bf16[256,1280]{1,0:T(8,128)(2,1)S(1)} collective-permute-done((bf16[256,1280]{1,0:T(8,128)(2,1)}, bf16[256,1280]{1,0:T(8,128)(2,1)S(1)}, u32[]{:S(2)}, u32[]{:S(2)}) %collective-permute-start.12) | collective-permute-done | bytes 655392 | tf_op jit(solution)/shard_map/ppermute | solution.py:311
  86.3 5.1 %collective-permute-start.16 = (bf16[256,1280]{1,0:T(8,128)(2,1)}, bf16[256,1280]{1,0:T(8,128)(2,1)}, u32[]{:S(2)}, u32[]{:S(2)}) collective-permute-start(bf16[256,1280]{1,0:T(8,128)(2,1)} %add.48), channel_id=1, source_target_pairs={{0,1},{1,2},{4,5},{5,6},{8,9},{9,10},{12,13},{13,14},{16,17},{17,1... | collective-permute-start | bytes 1966088 | tf_op jit(solution)/shard_map/ppermute | solution.py:311
  92.9 3.7 %collective-permute-start.8 = (bf16[512,1280]{1,0:T(8,128)(2,1)}, bf16[512,1280]{1,0:T(8,128)(2,1)}, u32[]{:S(2)}, u32[]{:S(2)}) collective-permute-start(bf16[512,1280]{1,0:T(8,128)(2,1)} %add.43), channel_id=1, source_target_pairs={{0,1},{1,2},{4,5},{5,6},{8,9},{9,10},{12,13},{13,14},{16,17},{17,1... | collective-permute-start | bytes 3932168 | tf_op jit(solution)/shard_map/ppermute | solution.py:311
  101.5 4.2 %all-to-all-start.2 = ((bf16[8,160,384]{2,1,0:T(8,128)(2,1)}), bf16[8,160,384]{2,1,0:T(8,128)(2,1)}, u32[]{:S(2)}, u32[]{:S(2)}) async-start(bf16[8,160,384]{2,1,0:T(8,128)(2,1)} %copy-done.2), calls=%async_computation.2 | async-start | bytes 1966080 | tf_op jit(solution)/shard_map/all_to_all | solution.py:308
  109.6 15.7 %shard_map.89 = (f32[160,2,16,320]{3,2,1,0:T(8,128)}, bf16[384,1280]{1,0:T(8,128)(2,1)}, bf16[384,1280]{1,0:T(8,128)(2,1)}, bf16[384,1280]{1,0:T(8,128)(2,1)}, b...) custom-call(s32[1280]{0:T(1024)} %wave.9, f32[16]{0:T(128)} %rate.7, ...), custom_call_target="tpu_custom_call", output_to_operand_aliasing={{0}: (6, {})} | custom-call | flops 1258291200 | bytes 24576000 | tf_op jit(solution)/shard_map/pallas_call | solution.py:133
  125.4 3.9 %collective-permute-start = (bf16[384,1280]{1,0:T(8,128)(2,1)}, bf16[384,1280]{1,0:T(8,128)(2,1)}, u32[]{:S(2)}, u32[]{:S(2)}) collective-permute-start(bf16[384,1280]{1,0:T(8,128)(2,1)} %get-tuple-element.33), channel_id=1, source_target_pairs={{3,2},{0,1},{7,6},{4,5},{11,10},{8,9},{15,14},{12,13},{19,18},{16,... | collective-permute-start | bytes 2949128 | tf_op jit(solution)/shard_map/ppermute | solution.py:311
  129.3 12.2 %collective-permute-done.15 = bf16[128,1280]{1,0:T(8,128)(2,1)} collective-permute-done((bf16[128,1280]{1,0:T(8,128)(2,1)}, bf16[128,1280]{1,0:T(8,128)(2,1)}, u32[]{:S(2)}, u32[]{:S(2)}) %collective-permute-start.15) | collective-permute-done | bytes 327712 | tf_op jit(solution)/shard_map/ppermute | solution.py:311
  148.8 4.2 %all-to-all-start.4 = ((bf16[8,160,384]{2,1,0:T(8,128)(2,1)}), bf16[8,160,384]{2,1,0:T(8,128)(2,1)}, u32[]{:S(2)}, u32[]{:S(2)}) async-start(bf16[8,160,384]{2,1,0:T(8,128)(2,1)} %copy-done.1), calls=%async_computation.4 | async-start | bytes 1966080 | tf_op jit(solution)/shard_map/all_to_all | solution.py:308
  153.7 3.2 %add.45 = bf16[512,1280]{1,0:T(8,128)(2,1)} add(bf16[512,1280]{1,0:T(8,128)(2,1)} %get-tuple-element.39, bf16[512,1280]{1,0:T(8,128)(2,1)} %collective-permute-done.8) | non-fusion elementwise | flops 655360 | bytes 3932160 | tf_op jit(solution)/shard_map/add | solution.py:327
  156.9 6.0 %collective-permute-start.9 = (bf16[512,1280]{1,0:T(8,128)(2,1)}, bf16[512,1280]{1,0:T(8,128)(2,1)}, u32[]{:S(2)}, u32[]{:S(2)}) collective-permute-start(bf16[512,1280]{1,0:T(8,128)(2,1)} %add.45), channel_id=1, source_target_pairs={{0,1},{1,2},{2,3},{4,5},{5,6},{6,7},{8,9},{9,10},{10,11},{12,13},{... | collective-permute-start | bytes 3932168 | tf_op jit(solution)/shard_map/ppermute | solution.py:311
  163.0 2.9 add.44
  167.3 2.5 add.40
  169.8 5.8 %collective-permute-start.3 = (bf16[384,1280]{1,0:T(8,128)(2,1)}, bf16[384,1280]{1,0:T(8,128)(2,1)}, u32[]{:S(2)}, u32[]{:S(2)}) collective-permute-start(bf16[384,1280]{1,0:T(8,128)(2,1)} %add.40), channel_id=1, source_target_pairs={{0,1},{1,2},{4,5},{5,6},{8,9},{9,10},{12,13},{13,14},{16,17},{17,1... | collective-permute-start | bytes 2949128 | tf_op jit(solution)/shard_map/ppermute | solution.py:311
  181.6 4.2 %all-to-all-start.3 = ((bf16[8,160,384]{2,1,0:T(8,128)(2,1)}), bf16[8,160,384]{2,1,0:T(8,128)(2,1)}, u32[]{:S(2)}, u32[]{:S(2)}) async-start(bf16[8,160,384]{2,1,0:T(8,128)(2,1)} %copy-done.4), calls=%async_computation.3 | async-start | bytes 1966080 | tf_op jit(solution)/shard_map/all_to_all | solution.py:308
  185.8 5.5 %collective-permute-done.9.refs_2_ = bf16[512,1280]{1,0:T(8,128)(2,1)} collective-permute-done((bf16[512,1280]{1,0:T(8,128)(2,1)}, bf16[512,1280]{1,0:T(8,128)(2,1)}, u32[]{:S(2)}, u32[]{:S(2)}) %collective-permute-start.9) | collective-permute-done | bytes 1310752 | tf_op jit(solution)/shard_map/ppermute | solution.py:311
  191.4 8.0 %collective-permute-done.7.refs_1_ = bf16[512,1280]{1,0:T(8,128)(2,1)} collective-permute-done((bf16[512,1280]{1,0:T(8,128)(2,1)}, bf16[512,1280]{1,0:T(8,128)(2,1)}, u32[]{:S(2)}, u32[]{:S(2)}) %collective-permute-start.7) | collective-permute-done | bytes 1310752 | tf_op jit(solution)/shard_map/ppermute | solution.py:311
  200.7 5.0 %rows.6 = bf16[8,160,512]{2,1,0:T(8,128)(2,1)S(1)} custom-call(bf16[512,1280]{1,0:T(8,128)(2,1)S(1)} %copy-done.5, bf16[512,1280]{1,0:T(8,128)(2,1)} %collective-permute-done.7.refs_1_, bf16[512,1280]{1,0:T(8,128)(2,1)} %collective-permute-done.9.refs_2_, bf16[1280,1280]{1,0:T(8,128)(2,1)S(1)} %fusion.refs_3_.refs_1_), custom_call_target="tpu_custom_call" | custom-call | flops 1677721600 | bytes 8519680 | tf_op jit(solution)/shard_map/rows/pallas_call | solution.py:195
  206.7 4.3 %all-to-all-start.1 = ((bf16[8,160,512]{2,1,0:T(8,128)(2,1)}), bf16[8,160,512]{2,1,0:T(8,128)(2,1)}, u32[]{:S(2)}, u32[]{:S(2)}) async-start(bf16[8,160,512]{2,1,0:T(8,128)(2,1)} %copy-done), calls=%async_computation.1 | async-start | bytes 2621440 | tf_op jit(solution)/shard_map/all_to_all | solution.py:308
  213.6 5.4 %collective-permute-start.4 = (bf16[384,1280]{1,0:T(8,128)(2,1)S(1)}, bf16[384,1280]{1,0:T(8,128)(2,1)S(1)}, u32[]{:S(2)}, u32[]{:S(2)}) collective-permute-start(bf16[384,1280]{1,0:T(8,128)(2,1)S(1)} %add.42), channel_id=1, source_target_pairs={{0,1},{1,2},{2,3},{4,5},{5,6},{6,7},{8,9},{9,10},{10,11},{12,13},{... | collective-permute-start | bytes 2949128 | tf_op jit(solution)/shard_map/ppermute | solution.py:311
  221.7 6.7 %collective-permute-start.17 = (bf16[8,160,384]{2,1,0:T(8,128)(2,1)}, bf16[8,160,384]{2,1,0:T(8,128)(2,1)}, u32[]{:S(2)}, u32[]{:S(2)}) collective-permute-start(bf16[8,160,384]{2,1,0:T(8,128)(2,1)} %all-to-all-done.4), channel_id=1, source_target_pairs={{0,1},{1,2},{2,3},{4,5},{5,6},{6,7},{8,9},{9,10},{10,11},{12,13},{... | collective-permute-start | bytes 2949128 | tf_op jit(solution)/shard_map/ppermute | solution.py:311
  229.7 11.3 %collective-permute-done.4.refs_2_ = bf16[384,1280]{1,0:T(8,128)(2,1)S(1)} collective-permute-done((bf16[384,1280]{1,0:T(8,128)(2,1)S(1)}, bf16[384,1280]{1,0:T(8,128)(2,1)S(1)}, u32[]{:S(2)}, u32[]{:S(2)}) %collective-permute-start.4) | collective-permute-done | bytes 983072 | tf_op jit(solution)/shard_map/ppermute | solution.py:311
  241.0 7.1 %collective-permute-done.2.refs_1_ = bf16[384,1280]{1,0:T(8,128)(2,1)S(1)} collective-permute-done((bf16[384,1280]{1,0:T(8,128)(2,1)S(1)}, bf16[384,1280]{1,0:T(8,128)(2,1)S(1)}, u32[]{:S(2)}, u32[]{:S(2)}) %collective-permute-start.2) | collective-permute-done | bytes 983072 | tf_op jit(solution)/shard_map/ppermute | solution.py:311
  251.3 4.0 %all-to-all-start = ((bf16[8,160,384]{2,1,0:T(8,128)(2,1)}), bf16[8,160,384]{2,1,0:T(8,128)(2,1)S(1)}, u32[]{:S(2)}, u32[]{:S(2)}) async-start(bf16[8,160,384]{2,1,0:T(8,128)(2,1)} %copy-done.3), calls=%async_computation | async-start | bytes 1966080 | tf_op jit(solution)/shard_map/all_to_all | solution.py:308
  256.3 6.7 %table.5.refs_5_ = bf16[8,96,2560]{2,1,0:T(8,128)(2,1)} custom-call(s32[8,48,128]{2,1,0:T(8,128)} %broadcast_in_dim.8.wave), custom_call_target="tpu_custom_call" | custom-call | flops 15728640 | bytes 3932160 | tf_op jit(solution)/shard_map/table/pallas_call | solution.py:42
  263.9 6.8 %table.3.refs_1_ = bf16[8,96,2560]{2,1,0:T(8,128)(2,1)} custom-call(s32[8,48,128]{2,1,0:T(8,128)} %broadcast_in_dim.6.wave), custom_call_target="tpu_custom_call" | custom-call | flops 15728640 | bytes 3932160 | tf_op jit(solution)/shard_map/table/pallas_call | solution.py:42
  271.5 7.6 %table.4.refs_4_ = bf16[8,128,2560]{2,1,0:T(8,128)(2,1)} custom-call(s32[8,64,128]{2,1,0:T(8,128)} %broadcast_in_dim.7.wave), custom_call_target="tpu_custom_call" | custom-call | flops 20971520 | bytes 5242880 | tf_op jit(solution)/shard_map/table/pallas_call | solution.py:42
  279.1 12.9 %wave.10.refs_2_ = f32[4,160,2560]{2,1,0:T(8,128)} custom-call(bf16[8,160,512]{2,1,0:T(8,128)(2,1)} %all-to-all-done.1.refs_0_, bf16[8,160,384]{2,1,0:T(8,128)(2,1)} %all-to-all-done.2.refs_1_, bf16[8,160,384]{2,1,0:T(8,128)(2,1)} %collective-permute-done.14.refs_2_, bf16[8,160,384]{2,1,0:T(8,128)(2,1)} %collective-permute-done.17.refs_3_, ...), custom_call_target="tpu_custom_call" | custom-call | flops 5872025600 | bytes 12451840 | tf_op jit(solution)/shard_map/wave/pallas_call | solution.py:261
  293.0 9.5 %wave.11 = bf16[4,160,2560]{2,1,0:T(8,128)(2,1)} custom-call(bf16[8,160,384]{2,1,0:T(8,128)(2,1)} %copy-done.7, bf16[8,96,2560]{2,1,0:T(8,128)(2,1)} %table.3.refs_1_, f32[4,160,2560]{2,1,0:T(8,128)} %wave.10.refs_2_), custom_call_target="tpu_custom_call" | custom-call | flops 2516582400 | bytes 7208960 | tf_op jit(solution)/shard_map/wave/pallas_call | solution.py:261
  (89 shorter events, 46.3 us)
Async XLA Ops:
  18.2 27.1 %copy-start.18 = (s32[1280]{0:T(1024)S(1)}, s32[1280]{0:T(1024)}, u32[]{:S(2)}) copy-start(s32[1280]{0:T(1024)} %param.13) | copy-start | bytes 15364
  36.8 48.6 %copy-start.14 = (bf16[256,1280]{1,0:T(8,128)(2,1)S(1)}, bf16[256,1280]{1,0:T(8,128)(2,1)}, u32[]{:S(2)}) copy-start(bf16[256,1280]{1,0:T(8,128)(2,1)} %get-tuple-element.46) | copy-start | bytes 1966084
  36.8 54.7 %collective-permute-start.5 = (bf16[512,1280]{1,0:T(8,128)(2,1)}, bf16[512,1280]{1,0:T(8,128)(2,1)S(1)}, u32[]{:S(2)}, u32[]{:S(2)}) collective-permute-start(bf16[512,1280]{1,0:T(8,128)(2,1)} %get-tuple-element.38), channel_id=1, source_target_pairs={{3,2},{0,1},{7,6},{4,5},{11,10},{8,9},{15,14},{12,13},{19,18},{16,... | collective-permute-start | bytes 3932168 | tf_op jit(solution)/shard_map/ppermute | solution.py:311
  41.9 43.4 %collective-permute-start.12 = (bf16[256,1280]{1,0:T(8,128)(2,1)}, bf16[256,1280]{1,0:T(8,128)(2,1)S(1)}, u32[]{:S(2)}, u32[]{:S(2)}) collective-permute-start(bf16[256,1280]{1,0:T(8,128)(2,1)} %get-tuple-element.47), channel_id=1, source_target_pairs={{3,2},{0,1},{7,6},{4,5},{11,10},{8,9},{15,14},{12,13},{19,18},{16,... | collective-permute-start | bytes 1966088 | tf_op jit(solution)/shard_map/ppermute | solution.py:311
  43.2 62.5 %collective-permute-start.10 = (bf16[128,1280]{1,0:T(8,128)(2,1)}, bf16[128,1280]{1,0:T(8,128)(2,1)}, u32[]{:S(2)}, u32[]{:S(2)}) collective-permute-start(bf16[128,1280]{1,0:T(8,128)(2,1)} %get-tuple-element.44), channel_id=1, source_target_pairs={{3,2},{0,1},{7,6},{4,5},{11,10},{8,9},{15,14},{12,13},{19,18},{16,... | collective-permute-start | bytes 983048 | tf_op jit(solution)/shard_map/ppermute | solution.py:311
  45.3 46.2 %copy-start.9 = (bf16[512,1280]{1,0:T(8,128)(2,1)S(1)}, bf16[512,1280]{1,0:T(8,128)(2,1)}, u32[]{:S(2)}) copy-start(bf16[512,1280]{1,0:T(8,128)(2,1)} %get-tuple-element.37) | copy-start | bytes 3932164
  86.3 57.8 %collective-permute-start.16 = (bf16[256,1280]{1,0:T(8,128)(2,1)}, bf16[256,1280]{1,0:T(8,128)(2,1)}, u32[]{:S(2)}, u32[]{:S(2)}) collective-permute-start(bf16[256,1280]{1,0:T(8,128)(2,1)} %add.48), channel_id=1, source_target_pairs={{0,1},{1,2},{4,5},{5,6},{8,9},{9,10},{12,13},{13,14},{16,17},{17,1... | collective-permute-start | bytes 1966088 | tf_op jit(solution)/shard_map/ppermute | solution.py:311
  91.4 6.9 %copy-start.13 = (bf16[256,1280]{1,0:T(8,128)(2,1)S(1)}, bf16[256,1280]{1,0:T(8,128)(2,1)}, u32[]{:S(2)}) copy-start(bf16[256,1280]{1,0:T(8,128)(2,1)} %get-tuple-element.41) | copy-start | bytes 1966084
  91.4 6.9 %copy-start.16 = (bf16[128,1280]{1,0:T(8,128)(2,1)S(1)}, bf16[128,1280]{1,0:T(8,128)(2,1)}, u32[]{:S(2)}) copy-start(bf16[128,1280]{1,0:T(8,128)(2,1)} %get-tuple-element.40) | copy-start | bytes 983044
  92.9 60.8 %collective-permute-start.8 = (bf16[512,1280]{1,0:T(8,128)(2,1)}, bf16[512,1280]{1,0:T(8,128)(2,1)}, u32[]{:S(2)}, u32[]{:S(2)}) collective-permute-start(bf16[512,1280]{1,0:T(8,128)(2,1)} %add.43), channel_id=1, source_target_pairs={{0,1},{1,2},{4,5},{5,6},{8,9},{9,10},{12,13},{13,14},{16,17},{17,1... | collective-permute-start | bytes 3932168 | tf_op jit(solution)/shard_map/ppermute | solution.py:311
  96.6 66.3 %collective-permute-start.6 = (bf16[512,1280]{1,0:T(8,128)(2,1)}, bf16[512,1280]{1,0:T(8,128)(2,1)}, u32[]{:S(2)}, u32[]{:S(2)}) collective-permute-start(bf16[512,1280]{1,0:T(8,128)(2,1)} %add.43), channel_id=1, source_target_pairs={{2,1},{3,2},{6,5},{7,6},{10,9},{11,10},{14,13},{15,14},{18,17},{19... | collective-permute-start | bytes 3932168 | tf_op jit(solution)/shard_map/ppermute | solution.py:311
  101.5 47.2 %all-to-all-start.2 = ((bf16[8,160,384]{2,1,0:T(8,128)(2,1)}), bf16[8,160,384]{2,1,0:T(8,128)(2,1)}, u32[]{:S(2)}, u32[]{:S(2)}) async-start(bf16[8,160,384]{2,1,0:T(8,128)(2,1)} %copy-done.2), calls=%async_computation.2 | async-start | bytes 1966080 | tf_op jit(solution)/shard_map/all_to_all | solution.py:308
  107.6 33.8 %collective-permute-start.15 = (bf16[128,1280]{1,0:T(8,128)(2,1)}, bf16[128,1280]{1,0:T(8,128)(2,1)}, u32[]{:S(2)}, u32[]{:S(2)}) collective-permute-start(bf16[128,1280]{1,0:T(8,128)(2,1)} %add.46), channel_id=1, source_target_pairs={{0,1},{1,2},{4,5},{5,6},{8,9},{9,10},{12,13},{13,14},{16,17},{17,1... | collective-permute-start | bytes 983048 | tf_op jit(solution)/shard_map/ppermute | solution.py:311
  125.4 41.9 %collective-permute-start = (bf16[384,1280]{1,0:T(8,128)(2,1)}, bf16[384,1280]{1,0:T(8,128)(2,1)}, u32[]{:S(2)}, u32[]{:S(2)}) collective-permute-start(bf16[384,1280]{1,0:T(8,128)(2,1)} %get-tuple-element.33), channel_id=1, source_target_pairs={{3,2},{0,1},{7,6},{4,5},{11,10},{8,9},{15,14},{12,13},{19,18},{16,... | collective-permute-start | bytes 2949128 | tf_op jit(solution)/shard_map/ppermute | solution.py:311
  141.5 35.7 %collective-permute-start.13 = (bf16[256,1280]{1,0:T(8,128)(2,1)}, bf16[256,1280]{1,0:T(8,128)(2,1)}, u32[]{:S(2)}, u32[]{:S(2)}) collective-permute-start(bf16[256,1280]{1,0:T(8,128)(2,1)} %add.48), channel_id=1, source_target_pairs={{2,1},{3,2},{6,5},{7,6},{10,9},{11,10},{14,13},{15,14},{18,17},{19... | collective-permute-start | bytes 1966088 | tf_op jit(solution)/shard_map/ppermute | solution.py:311
  148.8 32.9 %all-to-all-start.4 = ((bf16[8,160,384]{2,1,0:T(8,128)(2,1)}), bf16[8,160,384]{2,1,0:T(8,128)(2,1)}, u32[]{:S(2)}, u32[]{:S(2)}) async-start(bf16[8,160,384]{2,1,0:T(8,128)(2,1)} %copy-done.1), calls=%async_computation.4 | async-start | bytes 1966080 | tf_op jit(solution)/shard_map/all_to_all | solution.py:308
  153.0 14.2 %collective-permute-start.11 = (bf16[128,1280]{1,0:T(8,128)(2,1)}, bf16[128,1280]{1,0:T(8,128)(2,1)S(1)}, u32[]{:S(2)}, u32[]{:S(2)}) collective-permute-start(bf16[128,1280]{1,0:T(8,128)(2,1)} %add.46), channel_id=1, source_target_pairs={{2,1},{3,2},{6,5},{7,6},{10,9},{11,10},{14,13},{15,14},{18,17},{19... | collective-permute-start | bytes 983048 | tf_op jit(solution)/shard_map/ppermute | solution.py:311
  153.7 9.3 %copy-start.8 = (bf16[512,1280]{1,0:T(8,128)(2,1)S(1)}, bf16[512,1280]{1,0:T(8,128)(2,1)}, u32[]{:S(2)}) copy-start(bf16[512,1280]{1,0:T(8,128)(2,1)} %get-tuple-element.36) | copy-start | bytes 3932164
  156.9 34.4 %collective-permute-start.9 = (bf16[512,1280]{1,0:T(8,128)(2,1)}, bf16[512,1280]{1,0:T(8,128)(2,1)}, u32[]{:S(2)}, u32[]{:S(2)}) collective-permute-start(bf16[512,1280]{1,0:T(8,128)(2,1)} %add.45), channel_id=1, source_target_pairs={{0,1},{1,2},{2,3},{4,5},{5,6},{6,7},{8,9},{9,10},{10,11},{12,13},{... | collective-permute-start | bytes 3932168 | tf_op jit(solution)/shard_map/ppermute | solution.py:311
  165.9 33.5 %collective-permute-start.7 = (bf16[512,1280]{1,0:T(8,128)(2,1)}, bf16[512,1280]{1,0:T(8,128)(2,1)}, u32[]{:S(2)}, u32[]{:S(2)}) collective-permute-start(bf16[512,1280]{1,0:T(8,128)(2,1)} %add.44), channel_id=1, source_target_pairs={{1,0},{2,1},{3,2},{5,4},{6,5},{7,6},{9,8},{10,9},{11,10},{13,12},{... | collective-permute-start | bytes 3932168 | tf_op jit(solution)/shard_map/ppermute | solution.py:311
  167.2 10.0 %copy-start.12 = (bf16[256,1280]{1,0:T(8,128)(2,1)S(1)}, bf16[256,1280]{1,0:T(8,128)(2,1)}, u32[]{:S(2)}) copy-start(bf16[256,1280]{1,0:T(8,128)(2,1)} %get-tuple-element.45) | copy-start | bytes 1966084
  169.8 42.1 %collective-permute-start.3 = (bf16[384,1280]{1,0:T(8,128)(2,1)}, bf16[384,1280]{1,0:T(8,128)(2,1)}, u32[]{:S(2)}, u32[]{:S(2)}) collective-permute-start(bf16[384,1280]{1,0:T(8,128)(2,1)} %add.40), channel_id=1, source_target_pairs={{0,1},{1,2},{4,5},{5,6},{8,9},{9,10},{12,13},{13,14},{16,17},{17,1... | collective-permute-start | bytes 2949128 | tf_op jit(solution)/shard_map/ppermute | solution.py:311
  175.6 43.4 %collective-permute-start.1 = (bf16[384,1280]{1,0:T(8,128)(2,1)}, bf16[384,1280]{1,0:T(8,128)(2,1)}, u32[]{:S(2)}, u32[]{:S(2)}) collective-permute-start(bf16[384,1280]{1,0:T(8,128)(2,1)} %add.40), channel_id=1, source_target_pairs={{2,1},{3,2},{6,5},{7,6},{10,9},{11,10},{14,13},{15,14},{18,17},{19... | collective-permute-start | bytes 2949128 | tf_op jit(solution)/shard_map/ppermute | solution.py:311
  181.6 25.1 %all-to-all-start.3 = ((bf16[8,160,384]{2,1,0:T(8,128)(2,1)}), bf16[8,160,384]{2,1,0:T(8,128)(2,1)}, u32[]{:S(2)}, u32[]{:S(2)}) async-start(bf16[8,160,384]{2,1,0:T(8,128)(2,1)} %copy-done.4), calls=%async_computation.3 | async-start | bytes 1966080 | tf_op jit(solution)/shard_map/all_to_all | solution.py:308
  206.7 44.6 %all-to-all-start.1 = ((bf16[8,160,512]{2,1,0:T(8,128)(2,1)}), bf16[8,160,512]{2,1,0:T(8,128)(2,1)}, u32[]{:S(2)}, u32[]{:S(2)}) async-start(bf16[8,160,512]{2,1,0:T(8,128)(2,1)} %copy-done), calls=%async_computation.1 | async-start | bytes 2621440 | tf_op jit(solution)/shard_map/all_to_all | solution.py:308
  211.0 8.0 %copy-start.10 = (bf16[384,1280]{1,0:T(8,128)(2,1)S(1)}, bf16[384,1280]{1,0:T(8,128)(2,1)}, u32[]{:S(2)}) copy-start(bf16[384,1280]{1,0:T(8,128)(2,1)} %get-tuple-element.31) | copy-start | bytes 2949124
  213.6 34.5 %copy-start.6 = (bf16[384,1280]{1,0:T(8,128)(2,1)S(1)}, bf16[384,1280]{1,0:T(8,128)(2,1)}, u32[]{:S(2)}) copy-start(bf16[384,1280]{1,0:T(8,128)(2,1)} %get-tuple-element.30.refs_0_) | copy-start | bytes 2949124
  213.6 27.4 %collective-permute-start.4 = (bf16[384,1280]{1,0:T(8,128)(2,1)S(1)}, bf16[384,1280]{1,0:T(8,128)(2,1)S(1)}, u32[]{:S(2)}, u32[]{:S(2)}) collective-permute-start(bf16[384,1280]{1,0:T(8,128)(2,1)S(1)} %add.42), channel_id=1, source_target_pairs={{0,1},{1,2},{2,3},{4,5},{5,6},{6,7},{8,9},{9,10},{10,11},{12,13},{... | collective-permute-start | bytes 2949128 | tf_op jit(solution)/shard_map/ppermute | solution.py:311
  220.4 27.7 %collective-permute-start.2 = (bf16[384,1280]{1,0:T(8,128)(2,1)S(1)}, bf16[384,1280]{1,0:T(8,128)(2,1)S(1)}, u32[]{:S(2)}, u32[]{:S(2)}) collective-permute-start(bf16[384,1280]{1,0:T(8,128)(2,1)S(1)} %add.41), channel_id=1, source_target_pairs={{1,0},{2,1},{3,2},{5,4},{6,5},{7,6},{9,8},{10,9},{11,10},{13,12},{... | collective-permute-start | bytes 2949128 | tf_op jit(solution)/shard_map/ppermute | solution.py:311
  221.7 57.4 %collective-permute-start.17 = (bf16[8,160,384]{2,1,0:T(8,128)(2,1)}, bf16[8,160,384]{2,1,0:T(8,128)(2,1)}, u32[]{:S(2)}, u32[]{:S(2)}) collective-permute-start(bf16[8,160,384]{2,1,0:T(8,128)(2,1)} %all-to-all-done.4), channel_id=1, source_target_pairs={{0,1},{1,2},{2,3},{4,5},{5,6},{6,7},{8,9},{9,10},{10,11},{12,13},{... | collective-permute-start | bytes 2949128 | tf_op jit(solution)/shard_map/ppermute | solution.py:311
  228.4 50.7 %collective-permute-start.14 = (bf16[8,160,384]{2,1,0:T(8,128)(2,1)}, bf16[8,160,384]{2,1,0:T(8,128)(2,1)}, u32[]{:S(2)}, u32[]{:S(2)}) collective-permute-start(bf16[8,160,384]{2,1,0:T(8,128)(2,1)} %all-to-all-done.3), channel_id=1, source_target_pairs={{1,0},{2,1},{3,2},{5,4},{6,5},{7,6},{9,8},{10,9},{11,10},{13,12},{... | collective-permute-start | bytes 2949128 | tf_op jit(solution)/shard_map/ppermute | solution.py:311
  251.3 40.7 %all-to-all-start = ((bf16[8,160,384]{2,1,0:T(8,128)(2,1)}), bf16[8,160,384]{2,1,0:T(8,128)(2,1)S(1)}, u32[]{:S(2)}, u32[]{:S(2)}) async-start(bf16[8,160,384]{2,1,0:T(8,128)(2,1)} %copy-done.3), calls=%async_computation | async-start | bytes 1966080 | tf_op jit(solution)/shard_map/all_to_all | solution.py:308
  (10 other events, 19.6 us)

commit v2 on v1

--- a/solution.py
+++ b/solution.py
@@ -347,10 +347,8 @@
         )
     spectra.append([tail_own, tail_low, tail_high])
     tables.append(table_group(by_owner[:, : firsts[HEAD[0]]], 2 * lat_count))
-    late = len(HEAD) - 1
-    rest = [q for q in range(len(spectra)) if q != late]
-    acc = wave_group(lv, [spectra[q] for q in rest], [tables[q] for q in rest], None, jnp.float32)
-    pattern = wave_group(lv, [spectra[late]], [tables[late]], acc, jnp.bfloat16)
+    acc = wave_group(lv, spectra[:1], tables[:1], None, jnp.float32)
+    pattern = wave_group(lv, spectra[1:], tables[1:], acc, jnp.bfloat16)
     return chain, pattern
 
 

time: 305 us -> 305 us (level)
  transfers between devices with their start and end apart: 23 -> 23, of which waited for: 7 -> 7; matrix products, arithmetic and copies ran while one was open for 8% -> 8% of each run, Pallas kernels for 21% -> 20%
where the time goes in v2:
time: 305 us; the launch traced here: 302 us
  Pallas kernels  109 us (36%)
  waiting for transfers between devices  84.3 us (28%)
  starting transfers between devices  77.5 us (25%)
  other arithmetic  20.8 us (7%)
  local copies, waits for them, and re-layouts  9.79 us (3%)
    ppermute x18, waiting for transfers between devices, send(): return lax.ppermute(value, 'lev', pairs)  84.3 us
    ppermute x18, starting transfers between devices, send(): return lax.ppermute(value, 'lev', pairs)  56.6 us
    pallas_call x4, Pallas kernels, legendre_group(): pl.pallas_call(functools.partial(legendre_kernel, first, slots, n_lev, lv...  51.9 us
    pallas_call x2, Pallas kernels, wave_group(): pl.pallas_call(functools.partial(wave_kernel, lv, tuple((len(xs) for xs i...  22.1 us
    pallas_call x3, Pallas kernels, table_group(): pl.pallas_call(functools.partial(table_kernel, width), grid=(owners,), in...  21.1 us
    all_to_all x5, starting transfers between devices, exchange(): lax.all_to_all(spectrum, 'ma', split_axis=0, concat_axis=0, tiled=True)  20.9 us
    pallas_call x5, Pallas kernels, rows_group(): pl.pallas_call(functools.partial(rows_kernel, lv), grid=(n_rows // chunk,...  13.6 us
    add x8, other arithmetic, body(): lows[g] = pieces[g][n_lev - dist] + from_above[g]  12.5 us
  transfers between devices with their start and end apart: 23, of which 7 were waited for; matrix products, arithmetic and copies ran while one was open for 8% of the time, Pallas kernels for 20%

profile of v2, /device:TPU:0, one launch (start us, length us, event | category | flops | bytes accessed | tf_op | source)
XLA Modules:
  0.0 302.1 jit_solution(10314583780103016710)
XLA Ops:
  0.6 6.7 %shard_map.86 = (f32[160,2,16,320]{3,2,1,0:T(8,128)}, bf16[128,1280]{1,0:T(8,128)(2,1)}, bf16[128,1280]{1,0:T(8,128)(2,1)}, bf16[128,1280]{1,0:T(8,128)(2,1)}, b...) custom-call(s32[1280]{0:T(1024)} %wave.9, f32[16]{0:T(128)} %rate.7, f32[320]{0:T(512)} %amp.7, ...), custom_call_target="tpu_custom_call" | custom-call | flops 419430400 | bytes 8192000 | tf_op jit(solution)/shard_map/pallas_call | solution.py:133
  7.3 10.9 %shard_map.87 = (f32[160,2,16,320]{3,2,1,0:T(8,128)}, bf16[256,1280]{1,0:T(8,128)(2,1)}, bf16[256,1280]{1,0:T(8,128)(2,1)}, bf16[256,1280]{1,0:T(8,128)(2,1)}, b...) custom-call(s32[1280]{0:T(1024)} %wave.9, f32[16]{0:T(128)} %rate.7, ...), custom_call_target="tpu_custom_call", output_to_operand_aliasing={{0}: (6, {})} | custom-call | flops 838860800 | bytes 16384000 | tf_op jit(solution)/shard_map/pallas_call | solution.py:133
  18.2 18.6 %shard_map.88 = (f32[160,2,16,320]{3,2,1,0:T(8,128)}, bf16[512,1280]{1,0:T(8,128)(2,1)}, bf16[512,1280]{1,0:T(8,128)(2,1)}, bf16[512,1280]{1,0:T(8,128)(2,1)}, b...) custom-call(s32[1280]{0:T(1024)} %wave.9, f32[16]{0:T(128)} %rate.7, ...), custom_call_target="tpu_custom_call", output_to_operand_aliasing={{0}: (6, {})} | custom-call | flops 1677721600 | bytes 32768000 | tf_op jit(solution)/shard_map/pallas_call | solution.py:133
  36.8 5.1 %collective-permute-start.13 = (bf16[512,1280]{1,0:T(8,128)(2,1)}, bf16[512,1280]{1,0:T(8,128)(2,1)S(1)}, u32[]{:S(2)}, u32[]{:S(2)}) collective-permute-start(bf16[512,1280]{1,0:T(8,128)(2,1)} %get-tuple-element.48), channel_id=1, source_target_pairs={{3,2},{0,1},{7,6},{4,5},{11,10},{8,9},{15,14},{12,13},{19,18},{16,... | collective-permute-start | bytes 3932168 | tf_op jit(solution)/shard_map/ppermute | solution.py:311
  45.9 39.4 %collective-permute-done.7 = bf16[256,1280]{1,0:T(8,128)(2,1)S(1)} collective-permute-done((bf16[256,1280]{1,0:T(8,128)(2,1)}, bf16[256,1280]{1,0:T(8,128)(2,1)S(1)}, u32[]{:S(2)}, u32[]{:S(2)}) %collective-permute-start.7) | collective-permute-done | bytes 655392 | tf_op jit(solution)/shard_map/ppermute | solution.py:311
  86.3 5.1 %collective-permute-start.11 = (bf16[256,1280]{1,0:T(8,128)(2,1)}, bf16[256,1280]{1,0:T(8,128)(2,1)}, u32[]{:S(2)}, u32[]{:S(2)}) collective-permute-start(bf16[256,1280]{1,0:T(8,128)(2,1)} %add.45), channel_id=1, source_target_pairs={{0,1},{1,2},{4,5},{5,6},{8,9},{9,10},{12,13},{13,14},{16,17},{17,1... | collective-permute-start | bytes 1966088 | tf_op jit(solution)/shard_map/ppermute | solution.py:311
  92.9 3.7 %collective-permute-start.16 = (bf16[512,1280]{1,0:T(8,128)(2,1)}, bf16[512,1280]{1,0:T(8,128)(2,1)}, u32[]{:S(2)}, u32[]{:S(2)}) collective-permute-start(bf16[512,1280]{1,0:T(8,128)(2,1)} %add.49), channel_id=1, source_target_pairs={{0,1},{1,2},{4,5},{5,6},{8,9},{9,10},{12,13},{13,14},{16,17},{17,1... | collective-permute-start | bytes 3932168 | tf_op jit(solution)/shard_map/ppermute | solution.py:311
  101.5 4.2 %all-to-all-start.1 = ((bf16[8,160,384]{2,1,0:T(8,128)(2,1)}), bf16[8,160,384]{2,1,0:T(8,128)(2,1)}, u32[]{:S(2)}, u32[]{:S(2)}) async-start(bf16[8,160,384]{2,1,0:T(8,128)(2,1)} %copy-done.2), calls=%async_computation.1 | async-start | bytes 1966080 | tf_op jit(solution)/shard_map/all_to_all | solution.py:308
  109.6 15.7 %shard_map.89 = (f32[160,2,16,320]{3,2,1,0:T(8,128)}, bf16[384,1280]{1,0:T(8,128)(2,1)}, bf16[384,1280]{1,0:T(8,128)(2,1)}, bf16[384,1280]{1,0:T(8,128)(2,1)}, b...) custom-call(s32[1280]{0:T(1024)} %wave.9, f32[16]{0:T(128)} %rate.7, ...), custom_call_target="tpu_custom_call", output_to_operand_aliasing={{0}: (6, {})} | custom-call | flops 1258291200 | bytes 24576000 | tf_op jit(solution)/shard_map/pallas_call | solution.py:133
  125.4 3.9 %collective-permute-start = (bf16[384,1280]{1,0:T(8,128)(2,1)}, bf16[384,1280]{1,0:T(8,128)(2,1)}, u32[]{:S(2)}, u32[]{:S(2)}) collective-permute-start(bf16[384,1280]{1,0:T(8,128)(2,1)} %get-tuple-element.33), channel_id=1, source_target_pairs={{3,2},{0,1},{7,6},{4,5},{11,10},{8,9},{15,14},{12,13},{19,18},{16,... | collective-permute-start | bytes 2949128 | tf_op jit(solution)/shard_map/ppermute | solution.py:311
  129.3 12.2 %collective-permute-done.10 = bf16[128,1280]{1,0:T(8,128)(2,1)} collective-permute-done((bf16[128,1280]{1,0:T(8,128)(2,1)}, bf16[128,1280]{1,0:T(8,128)(2,1)}, u32[]{:S(2)}, u32[]{:S(2)}) %collective-permute-start.10) | collective-permute-done | bytes 327712 | tf_op jit(solution)/shard_map/ppermute | solution.py:311
  148.8 4.2 %all-to-all-start.3 = ((bf16[8,160,384]{2,1,0:T(8,128)(2,1)}), bf16[8,160,384]{2,1,0:T(8,128)(2,1)}, u32[]{:S(2)}, u32[]{:S(2)}) async-start(bf16[8,160,384]{2,1,0:T(8,128)(2,1)} %copy-done.1), calls=%async_computation.3 | async-start | bytes 1966080 | tf_op jit(solution)/shard_map/all_to_all | solution.py:308
  153.7 3.2 %add.51 = bf16[512,1280]{1,0:T(8,128)(2,1)} add(bf16[512,1280]{1,0:T(8,128)(2,1)} %get-tuple-element.49, bf16[512,1280]{1,0:T(8,128)(2,1)} %collective-permute-done.16) | non-fusion elementwise | flops 655360 | bytes 3932160 | tf_op jit(solution)/shard_map/add | solution.py:327
  156.9 6.0 %collective-permute-start.17 = (bf16[512,1280]{1,0:T(8,128)(2,1)}, bf16[512,1280]{1,0:T(8,128)(2,1)}, u32[]{:S(2)}, u32[]{:S(2)}) collective-permute-start(bf16[512,1280]{1,0:T(8,128)(2,1)} %add.51), channel_id=1, source_target_pairs={{0,1},{1,2},{2,3},{4,5},{5,6},{6,7},{8,9},{9,10},{10,11},{12,13},{... | collective-permute-start | bytes 3932168 | tf_op jit(solution)/shard_map/ppermute | solution.py:311
  163.0 2.9 add.50
  167.3 2.5 add.40
  169.8 5.8 %collective-permute-start.3 = (bf16[384,1280]{1,0:T(8,128)(2,1)}, bf16[384,1280]{1,0:T(8,128)(2,1)}, u32[]{:S(2)}, u32[]{:S(2)}) collective-permute-start(bf16[384,1280]{1,0:T(8,128)(2,1)} %add.40), channel_id=1, source_target_pairs={{0,1},{1,2},{4,5},{5,6},{8,9},{9,10},{12,13},{13,14},{16,17},{17,1... | collective-permute-start | bytes 2949128 | tf_op jit(solution)/shard_map/ppermute | solution.py:311
  181.7 4.2 %all-to-all-start.2 = ((bf16[8,160,384]{2,1,0:T(8,128)(2,1)}), bf16[8,160,384]{2,1,0:T(8,128)(2,1)}, u32[]{:S(2)}, u32[]{:S(2)}) async-start(bf16[8,160,384]{2,1,0:T(8,128)(2,1)} %copy-done.4), calls=%async_computation.2 | async-start | bytes 1966080 | tf_op jit(solution)/shard_map/all_to_all | solution.py:308
  185.9 5.5 %collective-permute-done.17.refs_2_ = bf16[512,1280]{1,0:T(8,128)(2,1)} collective-permute-done((bf16[512,1280]{1,0:T(8,128)(2,1)}, bf16[512,1280]{1,0:T(8,128)(2,1)}, u32[]{:S(2)}, u32[]{:S(2)}) %collective-permute-start.17) | collective-permute-done | bytes 1310752 | tf_op jit(solution)/shard_map/ppermute | solution.py:311
  191.4 8.0 %collective-permute-done.15.refs_1_ = bf16[512,1280]{1,0:T(8,128)(2,1)} collective-permute-done((bf16[512,1280]{1,0:T(8,128)(2,1)}, bf16[512,1280]{1,0:T(8,128)(2,1)}, u32[]{:S(2)}, u32[]{:S(2)}) %collective-permute-start.15) | collective-permute-done | bytes 1310752 | tf_op jit(solution)/shard_map/ppermute | solution.py:311
  200.7 5.0 %rows.9 = bf16[8,160,512]{2,1,0:T(8,128)(2,1)S(1)} custom-call(bf16[512,1280]{1,0:T(8,128)(2,1)S(1)} %copy-done.5, bf16[512,1280]{1,0:T(8,128)(2,1)} %collective-permute-done.15.refs_1_, bf16[512,1280]{1,0:T(8,128)(2,1)} %collective-permute-done.17.refs_2_, bf16[1280,1280]{1,0:T(8,128)(2,1)S(1)} %fusion.refs_3_.refs_1_), custom_call_target="tpu_custom_call" | custom-call | flops 1677721600 | bytes 8519680 | tf_op jit(solution)/shard_map/rows/pallas_call | solution.py:195
  206.7 4.3 %all-to-all-start.4 = ((bf16[8,160,512]{2,1,0:T(8,128)(2,1)}), bf16[8,160,512]{2,1,0:T(8,128)(2,1)}, u32[]{:S(2)}, u32[]{:S(2)}) async-start(bf16[8,160,512]{2,1,0:T(8,128)(2,1)} %copy-done), calls=%async_computation.4 | async-start | bytes 2621440 | tf_op jit(solution)/shard_map/all_to_all | solution.py:308
  213.6 5.4 %collective-permute-start.4 = (bf16[384,1280]{1,0:T(8,128)(2,1)S(1)}, bf16[384,1280]{1,0:T(8,128)(2,1)S(1)}, u32[]{:S(2)}, u32[]{:S(2)}) collective-permute-start(bf16[384,1280]{1,0:T(8,128)(2,1)S(1)} %add.42), channel_id=1, source_target_pairs={{0,1},{1,2},{2,3},{4,5},{5,6},{6,7},{8,9},{9,10},{10,11},{12,13},{... | collective-permute-start | bytes 2949128 | tf_op jit(solution)/shard_map/ppermute | solution.py:311
  221.7 6.7 %collective-permute-start.12 = (bf16[8,160,384]{2,1,0:T(8,128)(2,1)}, bf16[8,160,384]{2,1,0:T(8,128)(2,1)}, u32[]{:S(2)}, u32[]{:S(2)}) collective-permute-start(bf16[8,160,384]{2,1,0:T(8,128)(2,1)} %all-to-all-done.3), channel_id=1, source_target_pairs={{0,1},{1,2},{2,3},{4,5},{5,6},{6,7},{8,9},{9,10},{10,11},{12,13},{... | collective-permute-start | bytes 2949128 | tf_op jit(solution)/shard_map/ppermute | solution.py:311
  229.7 11.3 %collective-permute-done.4.refs_2_ = bf16[384,1280]{1,0:T(8,128)(2,1)S(1)} collective-permute-done((bf16[384,1280]{1,0:T(8,128)(2,1)S(1)}, bf16[384,1280]{1,0:T(8,128)(2,1)S(1)}, u32[]{:S(2)}, u32[]{:S(2)}) %collective-permute-start.4) | collective-permute-done | bytes 983072 | tf_op jit(solution)/shard_map/ppermute | solution.py:311
  241.0 7.1 %collective-permute-done.2.refs_1_ = bf16[384,1280]{1,0:T(8,128)(2,1)S(1)} collective-permute-done((bf16[384,1280]{1,0:T(8,128)(2,1)S(1)}, bf16[384,1280]{1,0:T(8,128)(2,1)S(1)}, u32[]{:S(2)}, u32[]{:S(2)}) %collective-permute-start.2) | collective-permute-done | bytes 983072 | tf_op jit(solution)/shard_map/ppermute | solution.py:311
  251.4 4.0 %all-to-all-start = ((bf16[8,160,384]{2,1,0:T(8,128)(2,1)}), bf16[8,160,384]{2,1,0:T(8,128)(2,1)S(1)}, u32[]{:S(2)}, u32[]{:S(2)}) async-start(bf16[8,160,384]{2,1,0:T(8,128)(2,1)} %copy-done.3), calls=%async_computation | async-start | bytes 1966080 | tf_op jit(solution)/shard_map/all_to_all | solution.py:308
  256.4 6.8 %table.3.refs_4_ = bf16[8,96,2560]{2,1,0:T(8,128)(2,1)} custom-call(s32[8,48,128]{2,1,0:T(8,128)} %broadcast_in_dim.6.wave), custom_call_target="tpu_custom_call" | custom-call | flops 15728640 | bytes 3932160 | tf_op jit(solution)/shard_map/table/pallas_call | solution.py:42
  263.9 6.7 %table.4.refs_5_ = bf16[8,96,2560]{2,1,0:T(8,128)(2,1)} custom-call(s32[8,48,128]{2,1,0:T(8,128)} %broadcast_in_dim.7.wave), custom_call_target="tpu_custom_call" | custom-call | flops 15728640 | bytes 3932160 | tf_op jit(solution)/shard_map/table/pallas_call | solution.py:42
  271.5 7.6 %table.5.refs_1_ = bf16[8,128,2560]{2,1,0:T(8,128)(2,1)} custom-call(s32[8,64,128]{2,1,0:T(8,128)} %broadcast_in_dim.8.wave), custom_call_target="tpu_custom_call" | custom-call | flops 20971520 | bytes 5242880 | tf_op jit(solution)/shard_map/table/pallas_call | solution.py:42
  279.1 9.1 %wave.10.refs_6_ = f32[4,160,2560]{2,1,0:T(8,128)} custom-call(bf16[8,160,512]{2,1,0:T(8,128)(2,1)} %all-to-all-done.4.refs_0_, bf16[8,128,2560]{2,1,0:T(8,128)(2,1)} %table.5.refs_1_), custom_call_target="tpu_custom_call" | custom-call | flops 3355443200 | bytes 8519680 | tf_op jit(solution)/shard_map/wave/pallas_call | solution.py:261
  289.1 13.0 %wave.11 = bf16[4,160,2560]{2,1,0:T(8,128)(2,1)} custom-call(bf16[8,160,384]{2,1,0:T(8,128)(2,1)} %copy-done.7, bf16[8,160,384]{2,1,0:T(8,128)(2,1)} %all-to-all-done.1.refs_1_, bf16[8,160,384]{2,1,0:T(8,128)(2,1)} %collective-permute-done.9.refs_2_, bf16[8,160,384]{2,1,0:T(8,128)(2,1)} %collective-permute-done.12.refs_3_, ...), custom_call_target="tpu_custom_call" | custom-call | flops 5033164800 | bytes 11141120 | tf_op jit(solution)/shard_map/wave/pallas_call | solution.py:261
  (89 shorter events, 46.3 us)
Async XLA Ops:
  18.2 27.1 %copy-start.18 = (s32[1280]{0:T(1024)S(1)}, s32[1280]{0:T(1024)}, u32[]{:S(2)}) copy-start(s32[1280]{0:T(1024)} %param.13) | copy-start | bytes 15364
  36.8 48.6 %copy-start.14 = (bf16[256,1280]{1,0:T(8,128)(2,1)S(1)}, bf16[256,1280]{1,0:T(8,128)(2,1)}, u32[]{:S(2)}) copy-start(bf16[256,1280]{1,0:T(8,128)(2,1)} %get-tuple-element.41) | copy-start | bytes 1966084
  36.8 54.7 %collective-permute-start.13 = (bf16[512,1280]{1,0:T(8,128)(2,1)}, bf16[512,1280]{1,0:T(8,128)(2,1)S(1)}, u32[]{:S(2)}, u32[]{:S(2)}) collective-permute-start(bf16[512,1280]{1,0:T(8,128)(2,1)} %get-tuple-element.48), channel_id=1, source_target_pairs={{3,2},{0,1},{7,6},{4,5},{11,10},{8,9},{15,14},{12,13},{19,18},{16,... | collective-permute-start | bytes 3932168 | tf_op jit(solution)/shard_map/ppermute | solution.py:311
  41.9 43.4 %collective-permute-start.7 = (bf16[256,1280]{1,0:T(8,128)(2,1)}, bf16[256,1280]{1,0:T(8,128)(2,1)S(1)}, u32[]{:S(2)}, u32[]{:S(2)}) collective-permute-start(bf16[256,1280]{1,0:T(8,128)(2,1)} %get-tuple-element.42), channel_id=1, source_target_pairs={{3,2},{0,1},{7,6},{4,5},{11,10},{8,9},{15,14},{12,13},{19,18},{16,... | collective-permute-start | bytes 1966088 | tf_op jit(solution)/shard_map/ppermute | solution.py:311
  43.2 62.5 %collective-permute-start.5 = (bf16[128,1280]{1,0:T(8,128)(2,1)}, bf16[128,1280]{1,0:T(8,128)(2,1)}, u32[]{:S(2)}, u32[]{:S(2)}) collective-permute-start(bf16[128,1280]{1,0:T(8,128)(2,1)} %get-tuple-element.39), channel_id=1, source_target_pairs={{3,2},{0,1},{7,6},{4,5},{11,10},{8,9},{15,14},{12,13},{19,18},{16,... | collective-permute-start | bytes 983048 | tf_op jit(solution)/shard_map/ppermute | solution.py:311
  45.3 46.2 %copy-start.9 = (bf16[512,1280]{1,0:T(8,128)(2,1)S(1)}, bf16[512,1280]{1,0:T(8,128)(2,1)}, u32[]{:S(2)}) copy-start(bf16[512,1280]{1,0:T(8,128)(2,1)} %get-tuple-element.47) | copy-start | bytes 3932164
  86.3 57.8 %collective-permute-start.11 = (bf16[256,1280]{1,0:T(8,128)(2,1)}, bf16[256,1280]{1,0:T(8,128)(2,1)}, u32[]{:S(2)}, u32[]{:S(2)}) collective-permute-start(bf16[256,1280]{1,0:T(8,128)(2,1)} %add.45), channel_id=1, source_target_pairs={{0,1},{1,2},{4,5},{5,6},{8,9},{9,10},{12,13},{13,14},{16,17},{17,1... | collective-permute-start | bytes 1966088 | tf_op jit(solution)/shard_map/ppermute | solution.py:311
  91.4 6.9 %copy-start.13 = (bf16[256,1280]{1,0:T(8,128)(2,1)S(1)}, bf16[256,1280]{1,0:T(8,128)(2,1)}, u32[]{:S(2)}) copy-start(bf16[256,1280]{1,0:T(8,128)(2,1)} %get-tuple-element.36) | copy-start | bytes 1966084
  91.4 6.9 %copy-start.16 = (bf16[128,1280]{1,0:T(8,128)(2,1)S(1)}, bf16[128,1280]{1,0:T(8,128)(2,1)}, u32[]{:S(2)}) copy-start(bf16[128,1280]{1,0:T(8,128)(2,1)} %get-tuple-element.35) | copy-start | bytes 983044
  92.9 60.8 %collective-permute-start.16 = (bf16[512,1280]{1,0:T(8,128)(2,1)}, bf16[512,1280]{1,0:T(8,128)(2,1)}, u32[]{:S(2)}, u32[]{:S(2)}) collective-permute-start(bf16[512,1280]{1,0:T(8,128)(2,1)} %add.49), channel_id=1, source_target_pairs={{0,1},{1,2},{4,5},{5,6},{8,9},{9,10},{12,13},{13,14},{16,17},{17,1... | collective-permute-start | bytes 3932168 | tf_op jit(solution)/shard_map/ppermute | solution.py:311
  96.6 66.3 %collective-permute-start.14 = (bf16[512,1280]{1,0:T(8,128)(2,1)}, bf16[512,1280]{1,0:T(8,128)(2,1)}, u32[]{:S(2)}, u32[]{:S(2)}) collective-permute-start(bf16[512,1280]{1,0:T(8,128)(2,1)} %add.49), channel_id=1, source_target_pairs={{2,1},{3,2},{6,5},{7,6},{10,9},{11,10},{14,13},{15,14},{18,17},{19... | collective-permute-start | bytes 3932168 | tf_op jit(solution)/shard_map/ppermute | solution.py:311
  101.5 47.2 %all-to-all-start.1 = ((bf16[8,160,384]{2,1,0:T(8,128)(2,1)}), bf16[8,160,384]{2,1,0:T(8,128)(2,1)}, u32[]{:S(2)}, u32[]{:S(2)}) async-start(bf16[8,160,384]{2,1,0:T(8,128)(2,1)} %copy-done.2), calls=%async_computation.1 | async-start | bytes 1966080 | tf_op jit(solution)/shard_map/all_to_all | solution.py:308
  107.6 33.8 %collective-permute-start.10 = (bf16[128,1280]{1,0:T(8,128)(2,1)}, bf16[128,1280]{1,0:T(8,128)(2,1)}, u32[]{:S(2)}, u32[]{:S(2)}) collective-permute-start(bf16[128,1280]{1,0:T(8,128)(2,1)} %add.43), channel_id=1, source_target_pairs={{0,1},{1,2},{4,5},{5,6},{8,9},{9,10},{12,13},{13,14},{16,17},{17,1... | collective-permute-start | bytes 983048 | tf_op jit(solution)/shard_map/ppermute | solution.py:311
  125.4 41.9 %collective-permute-start = (bf16[384,1280]{1,0:T(8,128)(2,1)}, bf16[384,1280]{1,0:T(8,128)(2,1)}, u32[]{:S(2)}, u32[]{:S(2)}) collective-permute-start(bf16[384,1280]{1,0:T(8,128)(2,1)} %get-tuple-element.33), channel_id=1, source_target_pairs={{3,2},{0,1},{7,6},{4,5},{11,10},{8,9},{15,14},{12,13},{19,18},{16,... | collective-permute-start | bytes 2949128 | tf_op jit(solution)/shard_map/ppermute | solution.py:311
  141.5 35.7 %collective-permute-start.8 = (bf16[256,1280]{1,0:T(8,128)(2,1)}, bf16[256,1280]{1,0:T(8,128)(2,1)}, u32[]{:S(2)}, u32[]{:S(2)}) collective-permute-start(bf16[256,1280]{1,0:T(8,128)(2,1)} %add.45), channel_id=1, source_target_pairs={{2,1},{3,2},{6,5},{7,6},{10,9},{11,10},{14,13},{15,14},{18,17},{19... | collective-permute-start | bytes 1966088 | tf_op jit(solution)/shard_map/ppermute | solution.py:311
  148.8 32.9 %all-to-all-start.3 = ((bf16[8,160,384]{2,1,0:T(8,128)(2,1)}), bf16[8,160,384]{2,1,0:T(8,128)(2,1)}, u32[]{:S(2)}, u32[]{:S(2)}) async-start(bf16[8,160,384]{2,1,0:T(8,128)(2,1)} %copy-done.1), calls=%async_computation.3 | async-start | bytes 1966080 | tf_op jit(solution)/shard_map/all_to_all | solution.py:308
  153.0 14.2 %collective-permute-start.6 = (bf16[128,1280]{1,0:T(8,128)(2,1)}, bf16[128,1280]{1,0:T(8,128)(2,1)S(1)}, u32[]{:S(2)}, u32[]{:S(2)}) collective-permute-start(bf16[128,1280]{1,0:T(8,128)(2,1)} %add.43), channel_id=1, source_target_pairs={{2,1},{3,2},{6,5},{7,6},{10,9},{11,10},{14,13},{15,14},{18,17},{19... | collective-permute-start | bytes 983048 | tf_op jit(solution)/shard_map/ppermute | solution.py:311
  153.7 9.3 %copy-start.8 = (bf16[512,1280]{1,0:T(8,128)(2,1)S(1)}, bf16[512,1280]{1,0:T(8,128)(2,1)}, u32[]{:S(2)}) copy-start(bf16[512,1280]{1,0:T(8,128)(2,1)} %get-tuple-element.46) | copy-start | bytes 3932164
  156.9 34.4 %collective-permute-start.17 = (bf16[512,1280]{1,0:T(8,128)(2,1)}, bf16[512,1280]{1,0:T(8,128)(2,1)}, u32[]{:S(2)}, u32[]{:S(2)}) collective-permute-start(bf16[512,1280]{1,0:T(8,128)(2,1)} %add.51), channel_id=1, source_target_pairs={{0,1},{1,2},{2,3},{4,5},{5,6},{6,7},{8,9},{9,10},{10,11},{12,13},{... | collective-permute-start | bytes 3932168 | tf_op jit(solution)/shard_map/ppermute | solution.py:311
  165.9 33.5 %collective-permute-start.15 = (bf16[512,1280]{1,0:T(8,128)(2,1)}, bf16[512,1280]{1,0:T(8,128)(2,1)}, u32[]{:S(2)}, u32[]{:S(2)}) collective-permute-start(bf16[512,1280]{1,0:T(8,128)(2,1)} %add.50), channel_id=1, source_target_pairs={{1,0},{2,1},{3,2},{5,4},{6,5},{7,6},{9,8},{10,9},{11,10},{13,12},{... | collective-permute-start | bytes 3932168 | tf_op jit(solution)/shard_map/ppermute | solution.py:311
  167.2 10.1 %copy-start.12 = (bf16[256,1280]{1,0:T(8,128)(2,1)S(1)}, bf16[256,1280]{1,0:T(8,128)(2,1)}, u32[]{:S(2)}) copy-start(bf16[256,1280]{1,0:T(8,128)(2,1)} %get-tuple-element.40) | copy-start | bytes 1966084
  169.8 42.1 %collective-permute-start.3 = (bf16[384,1280]{1,0:T(8,128)(2,1)}, bf16[384,1280]{1,0:T(8,128)(2,1)}, u32[]{:S(2)}, u32[]{:S(2)}) collective-permute-start(bf16[384,1280]{1,0:T(8,128)(2,1)} %add.40), channel_id=1, source_target_pairs={{0,1},{1,2},{4,5},{5,6},{8,9},{9,10},{12,13},{13,14},{16,17},{17,1... | collective-permute-start | bytes 2949128 | tf_op jit(solution)/shard_map/ppermute | solution.py:311
  175.5 43.4 %collective-permute-start.1 = (bf16[384,1280]{1,0:T(8,128)(2,1)}, bf16[384,1280]{1,0:T(8,128)(2,1)}, u32[]{:S(2)}, u32[]{:S(2)}) collective-permute-start(bf16[384,1280]{1,0:T(8,128)(2,1)} %add.40), channel_id=1, source_target_pairs={{2,1},{3,2},{6,5},{7,6},{10,9},{11,10},{14,13},{15,14},{18,17},{19... | collective-permute-start | bytes 2949128 | tf_op jit(solution)/shard_map/ppermute | solution.py:311
  181.7 25.1 %all-to-all-start.2 = ((bf16[8,160,384]{2,1,0:T(8,128)(2,1)}), bf16[8,160,384]{2,1,0:T(8,128)(2,1)}, u32[]{:S(2)}, u32[]{:S(2)}) async-start(bf16[8,160,384]{2,1,0:T(8,128)(2,1)} %copy-done.4), calls=%async_computation.2 | async-start | bytes 1966080 | tf_op jit(solution)/shard_map/all_to_all | solution.py:308
  206.7 44.6 %all-to-all-start.4 = ((bf16[8,160,512]{2,1,0:T(8,128)(2,1)}), bf16[8,160,512]{2,1,0:T(8,128)(2,1)}, u32[]{:S(2)}, u32[]{:S(2)}) async-start(bf16[8,160,512]{2,1,0:T(8,128)(2,1)} %copy-done), calls=%async_computation.4 | async-start | bytes 2621440 | tf_op jit(solution)/shard_map/all_to_all | solution.py:308
  211.0 8.0 %copy-start.10 = (bf16[384,1280]{1,0:T(8,128)(2,1)S(1)}, bf16[384,1280]{1,0:T(8,128)(2,1)}, u32[]{:S(2)}) copy-start(bf16[384,1280]{1,0:T(8,128)(2,1)} %get-tuple-element.31) | copy-start | bytes 2949124
  213.6 34.5 %copy-start.6 = (bf16[384,1280]{1,0:T(8,128)(2,1)S(1)}, bf16[384,1280]{1,0:T(8,128)(2,1)}, u32[]{:S(2)}) copy-start(bf16[384,1280]{1,0:T(8,128)(2,1)} %get-tuple-element.30.refs_0_) | copy-start | bytes 2949124
  213.6 27.4 %collective-permute-start.4 = (bf16[384,1280]{1,0:T(8,128)(2,1)S(1)}, bf16[384,1280]{1,0:T(8,128)(2,1)S(1)}, u32[]{:S(2)}, u32[]{:S(2)}) collective-permute-start(bf16[384,1280]{1,0:T(8,128)(2,1)S(1)} %add.42), channel_id=1, source_target_pairs={{0,1},{1,2},{2,3},{4,5},{5,6},{6,7},{8,9},{9,10},{10,11},{12,13},{... | collective-permute-start | bytes 2949128 | tf_op jit(solution)/shard_map/ppermute | solution.py:311
  220.4 27.7 %collective-permute-start.2 = (bf16[384,1280]{1,0:T(8,128)(2,1)S(1)}, bf16[384,1280]{1,0:T(8,128)(2,1)S(1)}, u32[]{:S(2)}, u32[]{:S(2)}) collective-permute-start(bf16[384,1280]{1,0:T(8,128)(2,1)S(1)} %add.41), channel_id=1, source_target_pairs={{1,0},{2,1},{3,2},{5,4},{6,5},{7,6},{9,8},{10,9},{11,10},{13,12},{... | collective-permute-start | bytes 2949128 | tf_op jit(solution)/shard_map/ppermute | solution.py:311
  221.7 66.5 %collective-permute-start.12 = (bf16[8,160,384]{2,1,0:T(8,128)(2,1)}, bf16[8,160,384]{2,1,0:T(8,128)(2,1)}, u32[]{:S(2)}, u32[]{:S(2)}) collective-permute-start(bf16[8,160,384]{2,1,0:T(8,128)(2,1)} %all-to-all-done.3), channel_id=1, source_target_pairs={{0,1},{1,2},{2,3},{4,5},{5,6},{6,7},{8,9},{9,10},{10,11},{12,13},{... | collective-permute-start | bytes 2949128 | tf_op jit(solution)/shard_map/ppermute | solution.py:311
  228.4 59.8 %collective-permute-start.9 = (bf16[8,160,384]{2,1,0:T(8,128)(2,1)}, bf16[8,160,384]{2,1,0:T(8,128)(2,1)}, u32[]{:S(2)}, u32[]{:S(2)}) collective-permute-start(bf16[8,160,384]{2,1,0:T(8,128)(2,1)} %all-to-all-done.2), channel_id=1, source_target_pairs={{1,0},{2,1},{3,2},{5,4},{6,5},{7,6},{9,8},{10,9},{11,10},{13,12},{... | collective-permute-start | bytes 2949128 | tf_op jit(solution)/shard_map/ppermute | solution.py:311
  251.4 36.8 %all-to-all-start = ((bf16[8,160,384]{2,1,0:T(8,128)(2,1)}), bf16[8,160,384]{2,1,0:T(8,128)(2,1)S(1)}, u32[]{:S(2)}, u32[]{:S(2)}) async-start(bf16[8,160,384]{2,1,0:T(8,128)(2,1)} %copy-done.3), calls=%async_computation | async-start | bytes 1966080 | tf_op jit(solution)/shard_map/all_to_all | solution.py:308
  (10 other events, 19.6 us)
